TPU v7x, 16 devices: a whole 2x2x2 slice. The times are simulated.
16 devices in a mesh: dp: 2 (over z), tp: 8 (over y, x, core).
Axes of the slice: x: 2, y: 2, z: 2, core: 2. Of those that a mesh axis runs over, the one named last changes fastest.
Arguments:
- w_up: bfloat16 [2, 2048, 16384], P(None, None, 'tp')
- w_down: bfloat16 [2, 16384, 2048], P(None, 'tp')
- x_saved: bfloat16 [2, 2, 4096, 2048], P(None, 'dp')
- h_saved: bfloat16 [2, 2, 4096, 16384], P(None, 'dp', None, 'tp')
- grad_out: bfloat16 [2, 4096, 2048], P('dp')
Outputs:
- output 1: bfloat16 [2, 4096, 2048], P('dp')
- output 2: float32 [2, 2048, 16384], P(None, None, 'tp')
- output 3: float32 [2, 16384, 2048], P(None, 'tp')
All inputs are finite; a program needn't handle non-finite values.
Results may differ from a plain program's by a relative error of at most 0.0130822.
Values are sent between devices in bfloat16 or wider.
A program may use at most 1 GiB of HBM per device.

v0:
```python
import jax
import jax.numpy as jnp
from jax import lax
from jax.sharding import PartitionSpec as P


def gelu_parts(hidden):
    tanh_val = jnp.tanh(0.7978845608028654 * (hidden + 0.044715 * hidden * hidden * hidden))
    gelu_out = 0.5 * hidden * (1.0 + tanh_val)
    gelu_slope = 0.5 * (1.0 + tanh_val) + 0.5 * hidden * (1.0 - tanh_val * tanh_val) * 0.7978845608028654 * (1.0 + 0.134145 * hidden * hidden)
    return gelu_out, gelu_slope


def solution(mesh):
    def run_backward(w_up, w_down, x_saved, h_saved, grad_out):
        layer_count = w_up.shape[0]
        grad_cur = grad_out
        up_grads = {}
        down_grads = {}
        for layer_idx in reversed(range(layer_count)):
            gelu_out, gelu_slope = gelu_parts(h_saved[layer_idx].astype(jnp.float32))
            act_grad = jnp.einsum("bsd,fd->bsf", grad_cur, w_down[layer_idx], preferred_element_type=jnp.float32)
            hid_grad = (act_grad * gelu_slope).astype(jnp.bfloat16)
            part_sum = jnp.einsum("bsf,df->bsd", hid_grad, w_up[layer_idx], preferred_element_type=jnp.float32).astype(jnp.bfloat16)
            full_sum = lax.psum(part_sum, "tp")
            down_grads[layer_idx] = jnp.einsum("bsf,bsd->fd", gelu_out.astype(jnp.bfloat16), grad_cur, preferred_element_type=jnp.float32)
            up_grads[layer_idx] = jnp.einsum("bsd,bsf->df", x_saved[layer_idx], hid_grad, preferred_element_type=jnp.float32)
            grad_cur = (grad_cur.astype(jnp.float32) + full_sum.astype(jnp.float32)).astype(jnp.bfloat16)
        up_total = lax.psum(jnp.stack([up_grads[layer_idx] for layer_idx in range(layer_count)]), "dp")
        down_total = lax.psum(jnp.stack([down_grads[layer_idx] for layer_idx in range(layer_count)]), "dp")
        return grad_cur, up_total, down_total
    return jax.shard_map(run_backward, mesh=mesh, in_specs=(P(None, None, "tp"), P(None, "tp", None), P(None, "dp", None, None), P(None, "dp", None, "tp"), P("dp", None, None)), out_specs=(P("dp", None, None), P(None, None, "tp"), P(None, "tp", None)), check_vma=False)
```

profile of v0, /device:TPU:0, one launch (start us, length us, event | category | flops | bytes accessed | tf_op | source)
XLA Modules:
  0.0 2160.3 jit_solution(17045194663415769060)
XLA Ops:
  7.2 0.0 all-reduce.5.cloned.1.call-start
  7.2 65.3 %fusion.21 = bf16[4096,2048]{1,0:T(8,128)(2,1)} fusion(bf16[1,4096,2048]{2,1,0:T(8,128)(2,1)} %param.9, bf16[2,1,4096,2048]{3,2,1,0:T(8,128)(2,1)} %param.8, bf16[2,2048,2048]{2,1,0:T(8,128)(2,1)} %param.6), kind=kOutput, calls=%fused_computation.33 | convolution fusion | flops 34527510528 | bytes 58720256 | tf_op jit(solution)/shard_map/bsd,fd->bsf/dot_general | solution.py:22
  72.5 42.1 %convert_bitcast_fusion.3 = bf16[1,4096,2048]{2,1,0:T(8,128)(2,1)} fusion(bf16[4096,2048]{1,0:T(8,128)(2,1)} %fusion.21, bf16[2,2048,2048]{2,1,0:T(8,128)(2,1)} %param.5), kind=kOutput, calls=%fused_computation.79 | convolution fusion | flops 34368126976 | bytes 41943040 | tf_op jit(solution)/shard_map/bsf,df->bsd/dot_general | solution.py:24
  114.5 0.0 all-reduce.5.cloned.1.call-update
  114.6 0.0 all-reduce.7.cloned.1.call-start
  114.6 43.6 %fusion.79 = f32[1,2048,2048]{1,2,0:T(8,128)} fusion(bf16[4096,2048]{1,0:T(8,128)(2,1)} %fusion.21, bf16[2,1,4096,2048]{3,2,1,0:T(8,128)(2,1)} %param.7), kind=kOutput, calls=%fused_computation.85 | convolution fusion | flops 34359738368 | bytes 50331648 | tf_op jit(solution)/shard_map/bsd,bsf->df/dot_general | solution.py:27
  158.2 55.1 %fusion.66 = f32[1,2048,2048]{2,1,0:T(8,128)} fusion(bf16[1,4096,2048]{2,1,0:T(8,128)(2,1)} %param.9, bf16[2,1,4096,2048]{3,2,1,0:T(8,128)(2,1)} %param.8), kind=kOutput, calls=%fused_computation.82 | convolution fusion | flops 34443624448 | bytes 50331648 | tf_op jit(solution)/shard_map/bsf,bsd->fd/dot_general | solution.py:26
  213.3 114.1 %all-reduce.5.cloned.1.call-done = bf16[1,4096,2048]{2,1,0:T(8,128)(2,1)} async-done(((bf16[1,4096,2048]{2,1,0:T(8,128)(2,1)}), bf16[1,4096,2048]{2,1,0:T(8,128)(2,1)}) %all-reduce.5.cloned.1.call-update) | async-done | bytes 16777232 | tf_op jit(solution)/shard_map/psum | solution.py:25
  327.4 60.8 %fusion.35 = bf16[4096,2048]{1,0:T(8,128)(2,1)} fusion(bf16[2,1,4096,2048]{3,2,1,0:T(8,128)(2,1)} %param.8, bf16[2,2048,2048]{2,1,0:T(8,128)(2,1)} %param.6, bf16[1,4096,2048]{2,1,0:T(8,128)(2,1)} %all-reduce.5.cloned.1.call-done, bf16[1,4096,2048]{2,1,0:T(8,128)(2,1)} %param.9), kind=kOutput, calls=%fused_computation.47 | convolution fusion | flops 34561064960 | bytes 75497472 | tf_op jit(solution)/shard_map/bsd,fd->bsf/dot_general | solution.py:22
  388.2 42.2 %convert_bitcast_fusion.2 = bf16[1,4096,2048]{2,1,0:T(8,128)(2,1)} fusion(bf16[4096,2048]{1,0:T(8,128)(2,1)} %fusion.35, bf16[2,2048,2048]{2,1,0:T(8,128)(2,1)} %param.5), kind=kOutput, calls=%fused_computation.78 | convolution fusion | flops 34368126976 | bytes 41943040 | tf_op jit(solution)/shard_map/bsf,df->bsd/dot_general | solution.py:24
  430.4 0.0 all-reduce.7.cloned.1.call-update
  430.5 0.0 all-reduce.9.cloned.1.call-start
  430.5 44.1 %fusion.76 = f32[1,2048,2048]{1,2,0:T(8,128)} fusion(bf16[4096,2048]{1,0:T(8,128)(2,1)} %fusion.35, bf16[2,1,4096,2048]{3,2,1,0:T(8,128)(2,1)} %param.7), kind=kOutput, calls=%fused_computation.84 | convolution fusion | flops 34359738368 | bytes 50331648 | tf_op jit(solution)/shard_map/bsd,bsf->df/dot_general | solution.py:27
  474.6 0.0 slice-start
  474.6 23.7 %pad_maximum_fusion = f32[2,2048,2048]{1,2,0:T(8,128)} fusion(f32[1,2048,2048]{1,2,0:T(8,128)} %fusion.79, f32[1,2048,2048]{1,2,0:T(8,128)} %fusion.76), kind=kLoop, calls=%fused_computation.54 | loop fusion | flops 8388608 | bytes 67108864 | tf_op jit(solution)/shard_map/stack | solution.py:29
  498.4 0.0 slice-start.1
  498.4 0.0 slice-start.2
  498.4 0.0 slice-start.3
  498.4 57.0 %fusion.71 = f32[1,2048,2048]{2,1,0:T(8,128)} fusion(bf16[2,1,4096,2048]{3,2,1,0:T(8,128)(2,1)} %param.8, bf16[1,4096,2048]{2,1,0:T(8,128)(2,1)} %all-reduce.5.cloned.1.call-done, bf16[1,4096,2048]{2,1,0:T(8,128)(2,1)} %param.9), kind=kOutput, calls=%fused_computation.83 | convolution fusion | flops 34477178880 | bytes 67108864 | tf_op jit(solution)/shard_map/bsf,bsd->fd/dot_general | solution.py:26
  555.3 0.0 slice-done
  555.3 0.0 slice-done.1
  555.3 0.0 slice-done.2
  555.3 0.0 slice-done.3
  555.4 18.5 pad_maximum_fusion.1
  573.8 0.0 all-reduce.9.cloned.1.call-update
  573.9 66.6 %all-reduce.7.cloned.1.call-done = bf16[1,4096,2048]{2,1,0:T(8,128)(2,1)} async-done(((bf16[1,4096,2048]{2,1,0:T(8,128)(2,1)}), bf16[1,4096,2048]{2,1,0:T(8,128)(2,1)}) %all-reduce.7.cloned.1.call-update) | async-done | bytes 16777232 | tf_op jit(solution)/shard_map/psum | solution.py:25
  640.5 25.1 %add_convert_fusion = bf16[1,4096,2048]{2,1,0:T(8,128)(2,1)} fusion(bf16[1,4096,2048]{2,1,0:T(8,128)(2,1)} %all-reduce.7.cloned.1.call-done, bf16[1,4096,2048]{2,1,0:T(8,128)(2,1)} %all-reduce.5.cloned.1.call-done, bf16[1,4096,2048]{2,1,0:T(8,128)(2,1)} %param.9), kind=kLoop, calls=%fused_computation.56 | loop fusion | flops 67108864 | bytes 67108864 | tf_op jit(solution)/shard_map/convert_element_type | solution.py:28
  665.5 1431.3 %all-reduce.9.cloned.1.call-done = (f32[2,2048,2048]{1,2,0:T(8,128)}, f32[2,2048,2048]{2,1,0:T(8,128)}) async-done(((f32[2,2048,2048]{1,2,0:T(8,128)}, f32[2,2048,2048]{2,1,0:T(8,128)}), (f32[2,2048,2048]{1,2,0:T(8,128)}, f32[2,2048,2048]{2,1,0:T(8,128)})) %all-reduce.9.cloned.1.call-update) | async-done | bytes 67108880 | tf_op jit(solution)/shard_map/psum | solution.py:29
  2096.9 33.6 %copy.8 = f32[2,2048,2048]{2,1,0:T(8,128)} copy(f32[2,2048,2048]{1,2,0:T(8,128)} %get-tuple-element.6) | data formatting | bytes 67108864
  2130.5 23.2 %copy.13 = f32[2,2048,2048]{2,1,0:T(8,128)} copy(f32[2,2048,2048]{2,1,0:T(8,128)} %get-tuple-element.10) | data formatting | bytes 67108864
  (1 shorter events, 0.0 us)
Async XLA Ops:
  7.2 320.2 %all-reduce.5.cloned.1.call-start = ((), (), s32[]{:S(2)}) async-start(), calls=%async_computation | async-start | bytes 33554432 | tf_op jit(solution)/shard_map/psum | solution.py:25
  114.6 525.9 %all-reduce.7.cloned.1.call-start = ((), (), s32[]{:S(2)}) async-start(), calls=%async_computation.1 | async-start | bytes 33554432 | tf_op jit(solution)/shard_map/psum | solution.py:25
  430.5 1666.4 %all-reduce.9.cloned.1.call-start = ((), (), s32[]{:S(2)}) async-start(), calls=%async_computation.2 | async-start | bytes 134217728 | tf_op jit(solution)/shard_map/psum | solution.py:29
  474.6 80.7 %slice-start = ((s8[16777216]{0:T(1024)(128)(4,1)}), s8[4194304]{0:T(1024)(128)(4,1)S(1)}, s32[]{:S(2)}) async-start(s8[16777216]{0:T(1024)(128)(4,1)} %bitcast.174), calls=%async_computation.3 | async-start | bytes 8388608
  498.4 57.0 %slice-start.1 = ((s8[16777216]{0:T(1024)(128)(4,1)}), s8[4194304]{0:T(1024)(128)(4,1)S(1)}, s32[]{:S(2)}) async-start(s8[16777216]{0:T(1024)(128)(4,1)} %bitcast.174), calls=%async_computation.4 | async-start | bytes 8388608
  498.4 57.0 %slice-start.2 = ((s8[16777216]{0:T(1024)(128)(4,1)}), s8[4194304]{0:T(1024)(128)(4,1)S(1)}, s32[]{:S(2)}) async-start(s8[16777216]{0:T(1024)(128)(4,1)} %bitcast.174), calls=%async_computation.5 | async-start | bytes 8388608
  498.4 57.0 %slice-start.3 = ((s8[16777216]{0:T(1024)(128)(4,1)}), s8[4194304]{0:T(1024)(128)(4,1)S(1)}, s32[]{:S(2)}) async-start(s8[16777216]{0:T(1024)(128)(4,1)} %bitcast.174), calls=%async_computation.6 | async-start | bytes 8388608
Sparse Core Ops, SparseCore 0:
  114.7 212.6 all-reduce.4
  430.6 209.8 all-reduce.6
  643.6 1453.2 all-reduce.8
where the time goes:
time: 2170 us; the launch traced here: 2160 us
  waiting for transfers between devices  1610 us (74%)
  matrix products  410 us (19%)
  other arithmetic  67.3 us (3%)
  local copies, waits for them, and re-layouts  56.8 us (3%)
    psum x1, waiting for transfers between devices, run_backward(): lax.psum(jnp.stack([up_grads[layer_idx] for layer_idx in range(layer_coun...  1430 us
    psum x2, waiting for transfers between devices, run_backward(): full_sum = lax.psum(part_sum, 'tp')  181 us
    dot_general x2, matrix products, run_backward(): jnp.einsum('bsd,fd->bsf', grad_cur, w_down[layer_idx], preferred_element_...  126 us
    dot_general x2, matrix products, run_backward(): jnp.einsum('bsf,bsd->fd', gelu_out.astype(jnp.bfloat16), grad_cur, prefer...  112 us
    dot_general x2, matrix products, run_backward(): jnp.einsum('bsd,bsf->df', x_saved[layer_idx], hid_grad, preferred_element...  87.7 us
    dot_general x2, matrix products, run_backward(): jnp.einsum('bsf,df->bsd', hid_grad, w_up[layer_idx], preferred_element_ty...  84.3 us
    unnamed x10, local copies, waits for them, and re-layouts  56.8 us
  transfers between devices with their start and end apart: 3, of which 3 were waited for; matrix products, arithmetic and copies ran while one was open for 12% of the time, Pallas kernels for 0%

commit v1 on v0

v1 whole, which is shorter than its diff:
```python
import jax
import jax.numpy as jnp
from jax import lax
from jax.experimental import pallas as pl
from jax.experimental.pallas import tpu as pltpu
from jax.sharding import PartitionSpec as P

D = 2048
F = 2048
PIECE = 1024
BM = 512
BN = 1024
C0 = 0.7978845608028654
C1 = 0.7978845608028654 * 0.044715
C3 = 0.7978845608028654 * 0.134145
AXES = ("dp", "tp")
VMEM_LIMIT = 60 * 1024 * 1024
BF16 = jnp.bfloat16
NN = (((1,), (0,)), ((), ()))
NT = (((1,), (1,)), ((), ()))
TN = (((0,), (0,)), ((), ()))


def make_perm(fn):
    pairs = []
    for z in range(2):
        for y in range(2):
            for x in range(2):
                for c in range(2):
                    z2, y2, x2, c2 = fn(z, y, x, c)
                    pairs.append((z * 8 + (y * 2 + x) * 2 + c, z2 * 8 + (y2 * 2 + x2) * 2 + c2))
    return pairs


PERM_Z = make_perm(lambda z, y, x, c: (1 - z, y, x, c))
PERM_C = make_perm(lambda z, y, x, c: (z, y, x, 1 - c))
PERM_S1 = make_perm(lambda z, y, x, c: (z, y, 1 - x, c) if c == 0 else (z, 1 - y, x, c))
PERM_S2 = make_perm(lambda z, y, x, c: (z, 1 - y, x, c) if c == 0 else (z, y, 1 - x, c))


def send(value, pairs):
    return lax.ppermute(value, AXES, pairs)


def device_order():
    tp = lax.axis_index("tp")
    z = lax.axis_index("dp")
    y, x, c = tp // 4, (tp // 2) % 2, tp % 2
    first = c == 0
    blocks = [jnp.where(first, x, 2 + y), jnp.where(first, 1 - x, 3 - y), jnp.where(first, 2 + y, x), jnp.where(first, 3 - y, 1 - x)]
    return jnp.stack(blocks + [z, 1 - z]).astype(jnp.int32), jnp.where(first, y, x).astype(jnp.int32)


TOKEN = jax.ShapeDtypeStruct((8, 128), jnp.float32)
TOKEN_SPEC = pl.BlockSpec((8, 128), lambda *g: (0, 0))
ANY_SPEC = pl.BlockSpec(memory_space=pl.ANY)
MINE, THEIRS = 4, 5


def call(body, grid, ins, outs, flops, order, token, aliases=None):
    n_in, n_out = len(ins), len(outs)

    def wrapped(order_ref, *refs):
        token_out = refs[n_in + 1 + n_out]
        token_out[...] = jnp.zeros((8, 128), jnp.float32)
        body(refs[:n_in], refs[n_in + 1:n_in + 1 + n_out])

    return pl.pallas_call(
        wrapped,
        grid_spec=pltpu.PrefetchScalarGridSpec(
            num_scalar_prefetch=1, grid=grid,
            in_specs=[s for _, s in ins] + [ANY_SPEC],
            out_specs=[s for _, s in outs] + [TOKEN_SPEC]),
        out_shape=[s for s, _ in outs] + [TOKEN],
        input_output_aliases={} if aliases is None else {k + 1: v for k, v in aliases.items()},
        compiler_params=pltpu.CompilerParams(vmem_limit_bytes=VMEM_LIMIT),
        cost_estimate=pl.CostEstimate(flops=flops, bytes_accessed=60_000_000, transcendentals=0),
    )(order, *[a for a, _ in ins], token)


class Piece:
    def __init__(self, array, *lead):
        self.array = array
        self.lead = lead

    def spec(self, rows, cols, place):
        n = len(self.lead)

        def index(*args):
            order = args[-1]
            return tuple(order[k[0]] if isinstance(k, tuple) else k for k in self.lead) + place(*args)

        return (self.array, pl.BlockSpec((None,) * n + (rows, cols), index))


def parts(arr):
    return [Piece(arr, k) for k in range(arr.shape[0])]


def whole(*arrs):
    return [Piece(a) for a in arrs]


def natural(arr, *lead):
    return [Piece(arr, *lead, (k,)) for k in range(4)]


def join(refs, axis=0):
    return jnp.concatenate([r[...] for r in refs], axis=axis)


def hidden_grad(order, token, grad, hidden, w_down, layer, half):
    n = len(grad)
    cols = BN if half else F
    groups = n // 2

    def body(ins, outs):
        act = lax.dot_general(join(ins[:n]), ins[2 * n][...], NT, preferred_element_type=jnp.float32)
        h = join(ins[n:2 * n]).astype(jnp.float32)
        h2 = h * h
        t = jnp.tanh(h * (C0 + C1 * h2))
        s = 0.5 + 0.5 * t
        a = h * s
        slope = s + a * ((1.0 - t) * (C0 + C3 * h2))
        outs[0][...] = a.reshape(n, BM // n, BN).astype(BF16)
        d = (act * slope).reshape(n, BM // n, BN).astype(BF16)
        for k in range(groups):
            outs[1 + k][...] = d[2 * k:2 * k + 2]

    ins = [p.spec(BM // n, D, lambda j, i, o: (i, 0)) for p in grad]
    ins += [p.spec(BM // n, BN, lambda j, i, o: (i, j)) for p in hidden]
    ins.append((w_down, pl.BlockSpec((None, BN, D), lambda j, i, o: (layer, o[MINE] if half else j, 0))))

    def out(m):
        return (jax.ShapeDtypeStruct((m, PIECE, cols), BF16), pl.BlockSpec((m, BM // n, BN), lambda j, i, o: (0, i, j)))

    *res, tok = call(body, (cols // BN, n * PIECE // BM), ins, [out(n)] + [out(2)] * groups, 2 * n * PIECE * D * cols, order, token)
    return res[0], res[1:], tok


def hidden_again(order, token, x, w_up, layer, half):
    n = len(x)
    cols = BN if half else F

    def body(ins, outs):
        h = lax.dot_general(join(ins[:n]), ins[n][...], NN, preferred_element_type=jnp.float32)
        outs[0][...] = h.reshape(n, BM // n, BN).astype(BF16)

    ins = [p.spec(BM // n, D, lambda j, i, o: (i, 0)) for p in x]
    ins.append((w_up, pl.BlockSpec((None, D, BN), lambda j, i, o: (layer, 0, o[MINE] if half else j))))
    out = (jax.ShapeDtypeStruct((n, PIECE, cols), BF16), pl.BlockSpec((n, BM // n, BN), lambda j, i, o: (0, i, j)))
    return call(body, (cols // BN, n * PIECE // BM), ins, [out], 2 * n * PIECE * D * cols, order, token)


def back_term(order, token, d_mine, d_core, w_mine, w_core, layer):
    n = 2

    def body(ins, outs):
        left = jnp.concatenate([join(ins[:n]), join(ins[n:2 * n])], axis=1)
        acc = lax.dot_general(left, join(ins[2 * n:2 * n + 2], 1), NT, preferred_element_type=jnp.float32)
        for k in range(n):
            outs[k][...] = acc[k * (BM // n):(k + 1) * (BM // n)].astype(BF16)

    ins = [p.spec(BM // n, F, lambda j, i, o: (i, 0)) for p in parts(d_mine) + parts(d_core)]
    ins += [(w, pl.BlockSpec((None, BN, F), lambda j, i, o: (layer, j, 0))) for w in (w_mine, w_core)]
    outs = [(jax.ShapeDtypeStruct((PIECE, D), BF16), pl.BlockSpec((BM // n, BN), lambda j, i, o: (i, j)))] * n
    return call(body, (D // BN, n * PIECE // BM), ins, outs, 4 * n * PIECE * D * F, order, token)


def weight_grad(order, token, left, right, left_cols, right_cols, bn, ins_more, outs, add, aliases):
    n = len(left)
    (grid_i, at_i), (grid_j, at_j) = left_cols, right_cols

    def body(ins, outs):
        acc = lax.dot_general(join(ins[:n]), join(ins[n:2 * n]), TN, preferred_element_type=jnp.float32)
        if add:
            acc = acc + ins[2 * n][...]
        for o in outs:
            o[...] = acc

    ins = [p.spec(PIECE, BN, lambda i, j, o: (0, at_i(i, o))) for p in left]
    ins += [p.spec(PIECE, bn, lambda i, j, o: (0, at_j(j, o))) for p in right]
    return call(body, (grid_i, grid_j), ins + ins_more, outs, 2 * n * PIECE * grid_i * BN * grid_j * bn, order, token,
                None if aliases is None else {2 * n + k: v for k, v in aliases.items()})


STACK = jax.ShapeDtypeStruct((2, 2048, 2048), jnp.float32)


def weight_full(order, token, left, right, total, add):
    tile = pl.BlockSpec((None, BN, BN), lambda i, j, o: (0, i, j))
    step = (2, lambda k, o: k)
    return weight_grad(order, token, left, right, step, step, BN, [(total, tile if add else ANY_SPEC)], [(STACK, tile)], add, {0: 0})


def weight_half(order, token, left, right, down, prev):
    bn = 512
    if down:
        shape = jax.ShapeDtypeStruct((BN, D), jnp.float32)
        cols = ((1, lambda k, o: o[MINE] if prev is None else 0), (4, lambda k, o: k))
        at = lambda i, j, o: (1, o[MINE], j)
    else:
        shape = jax.ShapeDtypeStruct((D, BN), jnp.float32)
        cols = ((2, lambda k, o: k), (2, lambda k, o: 2 * o[MINE] + k if prev is None else k))
        at = lambda i, j, o: (1, i, 2 * o[MINE] + j)
    tile = pl.BlockSpec((BN, bn), lambda i, j, o: (i, j))
    outs = [(shape, tile)]
    if prev is not None:
        outs.append((STACK, pl.BlockSpec((None, BN, bn), at)))
    return weight_grad(order, token, left, right, *cols, bn, [] if prev is None else [(prev, tile)], outs, prev is not None, None)


def finish(order, token, pieces, down_in, up_in, down, up):
    def body(ins, outs):
        i = pl.program_id(0)
        for k in range(4):
            @pl.when(i // 2 == k)
            def _(k=k):
                outs[0][...] = ins[k][...]
        outs[1][...] = ins[4][...]
        outs[2][...] = ins[5][...]

    ins = [p.spec(BM, D, lambda i, o, k=k: (jnp.clip(i - 2 * k, 0, 1), 0)) for k, p in enumerate(pieces)]
    ins += [(down_in, pl.BlockSpec((128, D), lambda i, o: (i, 0))), (up_in, pl.BlockSpec((256, BN), lambda i, o: (i, 0)))]
    ins += [(down, ANY_SPEC), (up, ANY_SPEC)]
    outs = [(jax.ShapeDtypeStruct((4, PIECE, D), BF16), pl.BlockSpec((None, BM, D), lambda i, o: (o[i // 2], i % 2, 0))),
            (STACK, pl.BlockSpec((None, 128, D), lambda i, o: (1, 8 * o[THEIRS] + i, 0))),
            (STACK, pl.BlockSpec((None, 256, BN), lambda i, o: (1, i, o[THEIRS])))]
    return call(body, (8,), ins, outs, 1000, order, token, {6: 1, 7: 2})


def f32(v):
    return v.astype(jnp.float32)


def solution(mesh):
    def steps(w_up, w_down, x_saved, h_saved, grad_out):
        order, sub = device_order()
        tok = jnp.zeros((8, 128), jnp.float32)
        x_nat = x_saved.reshape(2, 4, PIECE, D)
        h_nat = h_saved.reshape(2, 4, PIECE, F)
        g_nat = grad_out.reshape(4, PIECE, D)

        def my_half(block, which):
            return lax.dynamic_slice(block, (which * BM, 0), (BM, D))

        def both_halves(mine, other):
            return jnp.where(sub == 0, jnp.concatenate([mine, other]), jnp.concatenate([other, mine]))

        def own_block(arr, *lead):
            idx = tuple(lead) + (order[0], 0, 0)
            return lax.dynamic_slice(arr, idx, (1,) * (len(lead) + 1) + (PIECE, D)).reshape(PIECE, D)

        def summed(p02, near, which):
            return f32(my_half(p02, which)) + f32(my_half(near, which))

        x1z = send(own_block(x_nat, 1), PERM_Z)
        w_core = send(w_up, PERM_C)
        g2mine = own_block(g_nat)
        g2z = send(g2mine, PERM_Z)
        g2 = natural(g_nat)
        a1, (dm, do), tok = hidden_grad(order, tok, g2, natural(h_nat, 1), w_down, 1, False)
        dc = send(do, PERM_C)
        down_h, tok = weight_half(order, tok, parts(a1), g2, True, None)
        x1c0 = send(x1z, PERM_C)
        x1s = send(x1z, PERM_S1)
        p02, p13, tok = back_term(order, tok, dm, dc, w_up, w_core, 1)
        near = send(p13, PERM_S1)
        up_h, tok = weight_half(order, tok, natural(x_nat, 1), parts(dm) + parts(do), False, None)
        x1c1 = send(x1s, PERM_C)
        x0z = send(own_block(x_nat, 0), PERM_Z)
        hp, tok = hidden_again(order, tok, whole(x1z, x1c0, x1s, x1c1), w_up, 1, True)
        g2c0 = send(g2z, PERM_C)
        g2s = send(g2z, PERM_S1)
        far = send(summed(p02, near, 1 - sub).astype(BF16), PERM_S2)
        apa, (dpa,), tok = hidden_grad(order, tok, whole(g2z, g2c0), [Piece(hp, 0), Piece(hp, 1)], w_down, 1, True)
        g2c1 = send(g2s, PERM_C)
        g1m0 = (f32(my_half(g2mine, sub)) + (summed(p02, near, sub) + f32(far))).astype(BF16)
        g1m2 = send(g1m0, PERM_S2)
        apb, (dpb,), tok = hidden_grad(order, tok, whole(g2s, g2c1), [Piece(hp, 2), Piece(hp, 3)], w_down, 1, True)
        g1mine = both_halves(g1m0, g1m2)
        g1s = send(g1mine, PERM_S1)
        g1c0 = send(g1mine, PERM_C)
        g1zp = send(g1mine, PERM_Z)
        down_h, down, tok = weight_half(order, tok, parts(apa) + parts(apb), whole(g2z, g2c0, g2s, g2c1), True, down_h)
        down_in = send(down_h, PERM_Z)
        up_h, up, tok = weight_half(order, tok, whole(x1z, x1c0, x1s, x1c1), parts(dpa) + parts(dpb), False, up_h)
        g1c1 = send(g1s, PERM_C)
        up_in = send(up_h, PERM_Z)

        g1 = whole(g1mine, g1s, g1c0, g1c1)
        a0, (dm, do), tok = hidden_grad(order, tok, g1, natural(h_nat, 0), w_down, 0, False)
        dc = send(do, PERM_C)
        x0c0 = send(x0z, PERM_C)
        x0s = send(x0z, PERM_S1)
        down, tok = weight_full(order, tok, parts(a0), g1, down, False)
        x0c1 = send(x0s, PERM_C)
        g1cp0 = send(g1zp, PERM_C)
        g1sp = send(g1zp, PERM_S1)
        p02, p13, tok = back_term(order, tok, dm, dc, w_up, w_core, 0)
        near = send(p13, PERM_S1)
        g1cp1 = send(g1sp, PERM_C)
        up, tok = weight_full(order, tok, natural(x_nat, 0), parts(dm) + parts(do), up, False)
        far = send(summed(p02, near, 1 - sub).astype(BF16), PERM_S2)
        hp, tok = hidden_again(order, tok, whole(x0z, x0c0, x0s, x0c1), w_up, 0, False)
        g0m0 = (f32(g1m0) + (summed(p02, near, sub) + f32(far))).astype(BF16)
        g0m2 = send(g0m0, PERM_S2)
        g1p = whole(g1zp, g1cp0, g1sp, g1cp1)
        ap, (dma, dmb), tok = hidden_grad(order, tok, g1p, parts(hp), w_down, 0, False)
        g0mine = both_halves(g0m0, g0m2)
        g0s = send(g0mine, PERM_S1)
        g0c0 = send(g0mine, PERM_C)
        down, tok = weight_full(order, tok, parts(ap), g1p, down, True)
        g0c1 = send(g0s, PERM_C)
        up, tok = weight_full(order, tok, whole(x0z, x0c0, x0s, x0c1), parts(dma) + parts(dmb), up, True)
        grad_in, down, up, tok = finish(order, tok, whole(g0mine, g0s, g0c0, g0c1), down_in, up_in, down, up)
        return grad_in.reshape(1, 4 * PIECE, D), up, down

    body = jax.shard_map(
        steps, mesh=mesh,
        in_specs=(P(None, None, "tp"), P(None, "tp", None), P(None, "dp", None, None), P(None, "dp", None, "tp"), P("dp", None, None)),
        out_specs=(P("dp", None, None), P(None, None, "tp"), P(None, "tp", None)), check_vma=False)
    shapes = ((2, D, 16384), (2, 16384, D), (2, 2, 4096, D), (2, 2, 4096, 16384), (2, 4096, D))
    jax.eval_shape(body, *[jax.ShapeDtypeStruct(s, BF16) for s in shapes])
    return body
```

time: 2170 us -> 1230 us (0.57)
  waiting for transfers between devices: 1610 us -> 473 us
  Pallas kernels: 0 us -> 678 us
  matrix products: 410 us -> 0 us
  other arithmetic: 67.3 us -> 23.3 us
  local copies, waits for them, and re-layouts: 56.8 us -> 14.4 us
  starting transfers between devices: 0.12 us -> 28.6 us
    psum x3 -> x0, waiting for transfers between devices: 1610 us -> none  [the longest x1 1430 us: run_backward(): lax.psum(jnp.stack([up_grads[layer_idx] for layer_idx in range(layer_coun...]
    pallas_call x0 -> x18, Pallas kernels: none -> 678 us  [call(): pl.pallas_call(wrapped, grid_spec=pltpu.PrefetchScalarGridSpec(num_scalar...]
    ppermute x0 -> x33, waiting for transfers between devices: none -> 473 us  [send(): return lax.ppermute(value, AXES, pairs)]
    dot_general x8 -> x0, matrix products: 410 us -> none  [the longest x2 126 us: run_backward(): jnp.einsum('bsd,fd->bsf', grad_cur, w_down[layer_idx], preferred_element_...]
    unnamed x10 -> x6, local copies, waits for them, and re-layouts: 56.8 us -> 0.01 us
    another operation x2 -> x0, other arithmetic: 42.2 us -> none  [the longest x1 23.7 us: run_backward(): jnp.stack([up_grads[layer_idx] for layer_idx in range(layer_count)])]
    ppermute x0 -> x33, starting transfers between devices: none -> 28.6 us  [send(): return lax.ppermute(value, AXES, pairs)]
  transfers between devices with their start and end apart: 3 -> 33, of which waited for: 3 -> 9; matrix products, arithmetic and copies ran while one was open for 12% -> 3% of each run, Pallas kernels for 0% -> 49%
where the time goes in v1:
time: 1230 us; the launch traced here: 1220 us
  Pallas kernels  678 us (55%)
  waiting for transfers between devices  473 us (38%)
  starting transfers between devices  28.6 us (2%)
  other arithmetic  23.3 us (2%)
  local copies, waits for them, and re-layouts  14.4 us (1%)
    pallas_call x18, Pallas kernels, call(): pl.pallas_call(wrapped, grid_spec=pltpu.PrefetchScalarGridSpec(num_scalar...  678 us
    ppermute x33, waiting for transfers between devices, send(): return lax.ppermute(value, AXES, pairs)  473 us
    ppermute x33, starting transfers between devices, send(): return lax.ppermute(value, AXES, pairs)  28.6 us
  transfers between devices with their start and end apart: 33, of which 9 were waited for; matrix products, arithmetic and copies ran while one was open for 3% of the time, Pallas kernels for 49%

profile of v1, /device:TPU:0, one launch (start us, length us, event | category | flops | bytes accessed | tf_op | source)
XLA Modules:
  0.0 1217.9 jit_solution(1325897210008902427)
XLA Ops:
  0.6 0.8 collective-permute-start.1
  1.4 0.7 stack.27.order_ref
  2.1 0.6 broadcast_in_dim.3.refs_9_
  2.6 58.7 %shard_map.76 = (bf16[4,1024,2048]{2,1,0:T(8,128)(2,1)}, bf16[2,1024,2048]{2,1,0:T(8,128)(2,1)}, bf16[2,1024,2048]{2,1,0:T(8,128)(2,1)}, f32[8,128]{1,0:T(8,128)}) custom-call(s32[6]{0:T(128)} %stack.27.order_ref, bf16[4,1024,2048]{2,1,0:T(8,128)(2,1)} %bitcast.36, bf16[4,1024,2048]{2,1,0:T(8,128)(2,1)} %bitcast.37, bf16[4,1024,2048]{2,1,0:T(8,128)(2,1)} %bitcast.38, ...), custom_call_target="tpu_custom_call" | custom-call | flops 34359738368 | bytes 60000000 | tf_op jit(solution)/shard_map/pallas_call | solution.py:68
  61.4 0.1 collective-permute-start
  61.5 8.4 dynamic-slice_bitcast_fusion
  69.9 3.0 collective-permute-start.8
  72.9 25.4 %shard_map.77 = (f32[1024,2048]{1,0:T(8,128)}, f32[8,128]{1,0:T(8,128)}) custom-call(s32[6]{0:T(128)} %stack.27.order_ref, bf16[4,1024,2048]{2,1,0:T(8,128)(2,1)} %get-tuple-element.54.refs_0_.refs_1_.refs_2_.refs_3_, bf16[4,1024,2048]{2,1,0:T(8,128)(2,1)} %get-tuple-element.54.refs_0_.refs_1_.refs_2_.refs_3_, ...), custom_call_target="tpu_custom_call" | custom-call | flops 17179869184 | bytes 60000000 | tf_op jit(solution)/shard_map/pallas_call | solution.py:68
  98.3 43.4 %shard_map.78 = (bf16[1024,2048]{1,0:T(8,128)(2,1)}, bf16[1024,2048]{1,0:T(8,128)(2,1)}, f32[8,128]{1,0:T(8,128)}) custom-call(s32[6]{0:T(128)} %stack.27.order_ref, bf16[2,1024,2048]{2,1,0:T(8,128)(2,1)} %get-tuple-element.52.refs_0_.refs_1_.refs_4_.refs_5_, bf16[2,1024,2048]{2,1,0:T(8,128)(2,1)} %get-tuple-element.52.refs_0_.refs_1_.refs_4_.refs_5_, ...), custom_call_target="tpu_custom_call" | custom-call | flops 34359738368 | bytes 60000000 | tf_op jit(solution)/shard_map/pallas_call | solution.py:68
  141.7 1.5 collective-permute-start.2
  143.2 4.8 dynamic-slice_bitcast_fusion.1
  148.0 0.4 collective-permute-start.12
  148.5 16.1 %collective-permute-done.8.refs_0_ = bf16[1024,2048]{1,0:T(8,128)(2,1)} collective-permute-done((bf16[1024,2048]{1,0:T(8,128)(2,1)}, bf16[1024,2048]{1,0:T(8,128)(2,1)}, u32[]{:S(2)}, u32[]{:S(2)}) %collective-permute-start.8) | collective-permute-done | bytes 4194336 | tf_op jit(solution)/shard_map/ppermute | solution.py:42
  164.6 1.9 collective-permute-start.10
  166.5 24.0 %collective-permute-done.2 = bf16[1024,2048]{1,0:T(8,128)(2,1)} collective-permute-done((bf16[1024,2048]{1,0:T(8,128)(2,1)}, bf16[1024,2048]{1,0:T(8,128)(2,1)}, u32[]{:S(2)}, u32[]{:S(2)}) %collective-permute-start.2) | collective-permute-done | bytes 4194336 | tf_op jit(solution)/shard_map/ppermute | solution.py:42
  190.6 3.0 add_convert_fusion.2
  193.6 1.5 collective-permute-start.3
  195.1 58.7 %collective-permute-done.12.refs_0_.refs_4_ = bf16[1024,2048]{1,0:T(8,128)(2,1)} collective-permute-done((bf16[1024,2048]{1,0:T(8,128)(2,1)}, bf16[1024,2048]{1,0:T(8,128)(2,1)}, u32[]{:S(2)}, u32[]{:S(2)}) %collective-permute-start.12) | collective-permute-done | bytes 4194336 | tf_op jit(solution)/shard_map/ppermute | solution.py:42
  253.9 1.7 collective-permute-start.14
  255.5 5.3 fusion
  260.9 1.6 collective-permute-start.4
  262.5 0.5 collective-permute-start.11
  263.0 46.6 %collective-permute-done.4 = bf16[512,2048]{1,0:T(8,128)(2,1)} collective-permute-done((bf16[512,2048]{1,0:T(8,128)(2,1)S(1)}, bf16[512,2048]{1,0:T(8,128)(2,1)}, u32[]{:S(2)}, u32[]{:S(2)}) %collective-permute-start.4) | collective-permute-done | bytes 2097184 | tf_op jit(solution)/shard_map/ppermute | solution.py:42
  309.5 5.2 maximum_select_fusion.refs_0_.refs_4_
  314.7 0.4 collective-permute-start.5
  315.1 10.3 collective-permute-done.14.refs_0_.refs_6_
  325.4 25.7 %shard_map.79 = (f32[2048,1024]{1,0:T(8,128)}, f32[8,128]{1,0:T(8,128)}) custom-call(s32[6]{0:T(128)} %stack.27.order_ref, bf16[2,4,1024,2048]{3,2,1,0:T(8,128)(2,1)} %bitcast.20, bf16[2,4,1024,2048]{3,2,1,0:T(8,128)(2,1)} %bitcast.21, bf16[2,4,1024,2048]{3,2,1,0:T(8,128)(2,1)} %bitcast.22, bf16[2,4,1024,2048]{3,2,1,0:T(8,128)(2,1)} %bitcast.23, ...), custom_call_target="tpu_custom_call" | custom-call | flops 17179869184 | bytes 60000000 | tf_op jit(solution)/shard_map/pallas_call | solution.py:68
  351.1 23.6 %shard_map.80 = (bf16[4,1024,1024]{2,1,0:T(8,128)(2,1)}, f32[8,128]{1,0:T(8,128)}) custom-call(s32[6]{0:T(128)} %stack.27.order_ref, bf16[1024,2048]{1,0:T(8,128)(2,1)} %collective-permute-done.8.refs_0_, bf16[1024,2048]{1,0:T(8,128)(2,1)} %collective-permute-done.9.refs_1_, bf16[1024,2048]{1,0:T(8,128)(2,1)} %collective-permute-done.10.refs_2_, ...), custom_call_target="tpu_custom_call" | custom-call | flops 17179869184 | bytes 60000000 | tf_op jit(solution)/shard_map/pallas_call | solution.py:68
  374.7 0.5 collective-permute-start.6
  375.2 0.0 collective-permute-start.7
  375.3 18.8 %shard_map.81 = (bf16[2,1024,1024]{2,1,0:T(8,128)(2,1)}, bf16[2,1024,1024]{2,1,0:T(8,128)(2,1)}, f32[8,128]{1,0:T(8,128)}) custom-call(s32[6]{0:T(128)} %stack.27.order_ref, bf16[1024,2048]{1,0:T(8,128)(2,1)} %collective-permute-done.12.refs_0_.refs_4_, bf16[1024,2048]{1,0:T(8,128)(2,1)} %collective-permute-done.13.refs_1_.refs_5_, ...), custom_call_target="tpu_custom_call" | custom-call | flops 8589934592 | bytes 60000000 | tf_op jit(solution)/shard_map/pallas_call | solution.py:68
  394.1 18.3 %shard_map.82 = (bf16[2,1024,1024]{2,1,0:T(8,128)(2,1)}, bf16[2,1024,1024]{2,1,0:T(8,128)(2,1)}, f32[8,128]{1,0:T(8,128)}) custom-call(s32[6]{0:T(128)} %stack.27.order_ref, bf16[1024,2048]{1,0:T(8,128)(2,1)} %collective-permute-done.14.refs_0_.refs_6_, bf16[1024,2048]{1,0:T(8,128)(2,1)} %collective-permute-done.15.refs_1_.refs_7_, ...), custom_call_target="tpu_custom_call" | custom-call | flops 8589934592 | bytes 60000000 | tf_op jit(solution)/shard_map/pallas_call | solution.py:68
  412.4 26.9 %shard_map.83 = (f32[1024,2048]{1,0:T(8,128)}, f32[2,2048,2048]{2,1,0:T(8,128)}, f32[8,128]{1,0:T(8,128)}) custom-call(s32[6]{0:T(128)} %stack.27.order_ref, bf16[2,1024,1024]{2,1,0:T(8,128)(2,1)} %get-tuple-element.67.refs_0_.refs_1_, bf16[2,1024,1024]{2,1,0:T(8,128)(2,1)} %get-tuple-element.67.refs_0_.refs_1_, ...), custom_call_target="tpu_custom_call" | custom-call | flops 17179869184 | bytes 60000000 | tf_op jit(solution)/shard_map/pallas_call | solution.py:68
  439.3 30.1 %shard_map.84 = (f32[2048,1024]{1,0:T(8,128)}, f32[2,2048,2048]{2,1,0:T(8,128)}, f32[8,128]{1,0:T(8,128)}) custom-call(s32[6]{0:T(128)} %stack.27.order_ref, bf16[1024,2048]{1,0:T(8,128)(2,1)} %collective-permute-done.8.refs_0_, bf16[1024,2048]{1,0:T(8,128)(2,1)} %collective-permute-done.9.refs_1_, bf16[1024,2048]{1,0:T(8,128)(2,1)} %collective-permute-done.10.refs_2_, ...), custom_call_target="tpu_custom_call" | custom-call | flops 17179869184 | bytes 60000000 | tf_op jit(solution)/shard_map/pallas_call | solution.py:68
  469.4 58.2 %shard_map.85 = (bf16[4,1024,2048]{2,1,0:T(8,128)(2,1)}, bf16[2,1024,2048]{2,1,0:T(8,128)(2,1)}, bf16[2,1024,2048]{2,1,0:T(8,128)(2,1)}, f32[8,128]{1,0:T(8,128)}) custom-call(s32[6]{0:T(128)} %stack.27.order_ref, bf16[1024,2048]{1,0:T(8,128)(2,1)} %maximum_select_fusion.refs_0_.refs_4_, bf16[1024,2048]{1,0:T(8,128)(2,1)} %collective-permute-done.5.refs_1_.refs_5_, ...), custom_call_target="tpu_custom_call" | custom-call | flops 34359738368 | bytes 60000000 | tf_op jit(solution)/shard_map/pallas_call | solution.py:68
  527.6 0.5 collective-permute-start.16
  528.1 1.5 collective-permute-start.29
  529.6 0.5 collective-permute-start.25
  530.1 44.1 %shard_map.86 = (f32[2,2048,2048]{2,1,0:T(8,128)}, f32[8,128]{1,0:T(8,128)}) custom-call(s32[6]{0:T(128)} %stack.27.order_ref, bf16[4,1024,2048]{2,1,0:T(8,128)(2,1)} %get-tuple-element.75.refs_0_.refs_1_.refs_2_.refs_3_, bf16[4,1024,2048]{2,1,0:T(8,128)(2,1)} %get-tuple-element.75.refs_0_.refs_1_.refs_2_.refs_3_, ...), custom_call_target="tpu_custom_call", output_to_operand_aliasing={{0}: (9, {})} | custom-call | flops 34359738368 | bytes 60000000 | tf_op jit(solution)/shard_map/pallas_call | solution.py:68
  574.2 43.4 %shard_map.87 = (bf16[1024,2048]{1,0:T(8,128)(2,1)}, bf16[1024,2048]{1,0:T(8,128)(2,1)}, f32[8,128]{1,0:T(8,128)}) custom-call(s32[6]{0:T(128)} %stack.27.order_ref, bf16[2,1024,2048]{2,1,0:T(8,128)(2,1)} %get-tuple-element.73.refs_0_.refs_1_.refs_4_.refs_5_, bf16[2,1024,2048]{2,1,0:T(8,128)(2,1)} %get-tuple-element.73.refs_0_.refs_1_.refs_4_.refs_5_, ...), custom_call_target="tpu_custom_call" | custom-call | flops 34359738368 | bytes 60000000 | tf_op jit(solution)/shard_map/pallas_call | solution.py:68
  617.5 1.5 collective-permute-start.17
  619.1 2.8 collective-permute-done.29.refs_0_
  621.8 1.5 collective-permute-start.31
  623.3 87.5 %collective-permute-done.25.refs_0_.refs_4_ = bf16[1024,2048]{1,0:T(8,128)(2,1)} collective-permute-done((bf16[1024,2048]{1,0:T(8,128)(2,1)}, bf16[1024,2048]{1,0:T(8,128)(2,1)}, u32[]{:S(2)}, u32[]{:S(2)}) %collective-permute-start.25) | collective-permute-done | bytes 4194336 | tf_op jit(solution)/shard_map/ppermute | solution.py:42
  710.8 1.5 collective-permute-start.27
  712.3 2.4 add_convert_fusion.1
  714.7 1.5 collective-permute-start.18
  716.2 0.5 collective-permute-start.32
  716.7 65.4 %collective-permute-done.27.refs_2_.refs_6_ = bf16[1024,2048]{1,0:T(8,128)(2,1)} collective-permute-done((bf16[1024,2048]{1,0:T(8,128)(2,1)}, bf16[1024,2048]{1,0:T(8,128)(2,1)}, u32[]{:S(2)}, u32[]{:S(2)}) %collective-permute-start.27) | collective-permute-done | bytes 4194336 | tf_op jit(solution)/shard_map/ppermute | solution.py:42
  782.1 1.8 add_convert_fusion
  784.0 1.5 collective-permute-start.19
  785.5 44.2 %shard_map.88 = (f32[2,2048,2048]{2,1,0:T(8,128)}, f32[8,128]{1,0:T(8,128)}) custom-call(s32[6]{0:T(128)} %stack.27.order_ref, bf16[2,4,1024,2048]{3,2,1,0:T(8,128)(2,1)} %bitcast.24, bf16[2,4,1024,2048]{3,2,1,0:T(8,128)(2,1)} %bitcast.25, bf16[2,4,1024,2048]{3,2,1,0:T(8,128)(2,1)} %bitcast.26, ...), custom_call_target="tpu_custom_call", output_to_operand_aliasing={{0}: (9, {})} | custom-call | flops 34359738368 | bytes 60000000 | tf_op jit(solution)/shard_map/pallas_call | solution.py:68
  829.7 1.6 collective-permute-start.24
  831.3 5.6 maximum_select_fusion.1.refs_0_
  836.8 0.5 collective-permute-start.23
  837.3 1.5 collective-permute-start.20
  838.8 43.3 %shard_map.89 = (bf16[4,1024,2048]{2,1,0:T(8,128)(2,1)}, f32[8,128]{1,0:T(8,128)}) custom-call(s32[6]{0:T(128)} %stack.27.order_ref, bf16[1024,2048]{1,0:T(8,128)(2,1)} %collective-permute-done.29.refs_0_, bf16[1024,2048]{1,0:T(8,128)(2,1)} %collective-permute-done.30.refs_1_, bf16[1024,2048]{1,0:T(8,128)(2,1)} %collective-permute-done.31.refs_2_, ...), custom_call_target="tpu_custom_call" | custom-call | flops 34359738368 | bytes 60000000 | tf_op jit(solution)/shard_map/pallas_call | solution.py:68
  882.1 57.6 %shard_map.90 = (bf16[4,1024,2048]{2,1,0:T(8,128)(2,1)}, bf16[2,1024,2048]{2,1,0:T(8,128)(2,1)}, bf16[2,1024,2048]{2,1,0:T(8,128)(2,1)}, f32[8,128]{1,0:T(8,128)}) custom-call(s32[6]{0:T(128)} %stack.27.order_ref, bf16[1024,2048]{1,0:T(8,128)(2,1)} %collective-permute-done.25.refs_0_.refs_4_, bf16[1024,2048]{1,0:T(8,128)(2,1)} %collective-permute-done.26.refs_1_.refs_5_, ...), custom_call_target="tpu_custom_call" | custom-call | flops 34359738368 | bytes 60000000 | tf_op jit(solution)/shard_map/pallas_call | solution.py:68
  939.7 0.0 collective-permute-start.21
  939.8 0.5 collective-permute-start.22
  940.3 45.3 %shard_map.91 = (f32[2,2048,2048]{2,1,0:T(8,128)}, f32[8,128]{1,0:T(8,128)}) custom-call(s32[6]{0:T(128)} %stack.27.order_ref, bf16[4,1024,2048]{2,1,0:T(8,128)(2,1)} %get-tuple-element.88.refs_0_.refs_1_.refs_2_.refs_3_, bf16[4,1024,2048]{2,1,0:T(8,128)(2,1)} %get-tuple-element.88.refs_0_.refs_1_.refs_2_.refs_3_, ...), custom_call_target="tpu_custom_call", output_to_operand_aliasing={{0}: (9, {})} | custom-call | flops 34359738368 | bytes 60000000 | tf_op jit(solution)/shard_map/pallas_call | solution.py:68
  985.6 45.5 %shard_map.92 = (f32[2,2048,2048]{2,1,0:T(8,128)}, f32[8,128]{1,0:T(8,128)}) custom-call(s32[6]{0:T(128)} %stack.27.order_ref, bf16[1024,2048]{1,0:T(8,128)(2,1)} %collective-permute-done.29.refs_0_, bf16[1024,2048]{1,0:T(8,128)(2,1)} %collective-permute-done.30.refs_1_, ...), custom_call_target="tpu_custom_call", output_to_operand_aliasing={{0}: (9, {})} | custom-call | flops 34359738368 | bytes 60000000 | tf_op jit(solution)/shard_map/pallas_call | solution.py:68
  1031.1 161.3 %collective-permute-done.23.refs_4_ = f32[1024,2048]{1,0:T(8,128)} collective-permute-done((f32[1024,2048]{1,0:T(8,128)}, f32[1024,2048]{1,0:T(8,128)}, u32[]{:S(2)}, u32[]{:S(2)}) %collective-permute-start.23) | collective-permute-done | bytes 8388640 | tf_op jit(solution)/shard_map/ppermute | solution.py:42
  1192.4 25.4 %shard_map.93 = (bf16[4,1024,2048]{2,1,0:T(8,128)(2,1)}, f32[2,2048,2048]{2,1,0:T(8,128)}, f32[2,2048,2048]{2,1,0:T(8,128)}, f32[8,128]{1,0:T(8,128)}) custom-call(s32[6]{0:T(128)} %stack.27.order_ref, bf16[1024,2048]{1,0:T(8,128)(2,1)} %maximum_select_fusion.1.refs_0_, ...), custom_call_target="tpu_custom_call", output_to_operand_aliasing={{1}: (7, {}), {2}: (8, {})} | custom-call | flops 1000 | bytes 60000000 | tf_op jit(solution)/shard_map/pallas_call | solution.py:68
  (36 shorter events, 0.1 us)
Async XLA Ops:
  0.6 97.7 %collective-permute-start.1 = (bf16[2,2048,2048]{2,1,0:T(8,128)(2,1)}, bf16[2,2048,2048]{2,1,0:T(8,128)(2,1)}, u32[]{:S(2)}, u32[]{:S(2)}) collective-permute-start(bf16[2,2048,2048]{2,1,0:T(8,128)(2,1)} %refs_4_.11), channel_id=1, source_target_pairs={{0,1},{1,0},{2,3},{3,2},{4,5},{5,4},{6,7},{7,6},{8,9},{9,8},{10,11... | collective-permute-start | bytes 50331656 | tf_op jit(solution)/shard_map/ppermute | solution.py:42
  61.4 36.9 %collective-permute-start = (bf16[2,1024,2048]{2,1,0:T(8,128)(2,1)}, bf16[2,1024,2048]{2,1,0:T(8,128)(2,1)}, u32[]{:S(2)}, u32[]{:S(2)}) collective-permute-start(bf16[2,1024,2048]{2,1,0:T(8,128)(2,1)} %get-tuple-element.53.refs_6_.refs_7_), channel_id=1, source_target_pairs={{0,1},{1,0},{2,3},{3,2},{4,5},{5,4},{6,7},{7,6},{8,9},{9,8},{10,11... | collective-permute-start | bytes 25165832 | tf_op jit(solution)/shard_map/ppermute | solution.py:42
  69.9 94.7 %collective-permute-start.8 = (bf16[1024,2048]{1,0:T(8,128)(2,1)}, bf16[1024,2048]{1,0:T(8,128)(2,1)}, u32[]{:S(2)}, u32[]{:S(2)}) collective-permute-start(bf16[1024,2048]{1,0:T(8,128)(2,1)} %get-tuple-element.102), channel_id=1, source_target_pairs={{0,8},{1,9},{2,10},{3,11},{4,12},{5,13},{6,14},{7,15},{8,0},{9,1},... | collective-permute-start | bytes 12582920 | tf_op jit(solution)/shard_map/ppermute | solution.py:42
  141.7 48.9 %collective-permute-start.2 = (bf16[1024,2048]{1,0:T(8,128)(2,1)}, bf16[1024,2048]{1,0:T(8,128)(2,1)}, u32[]{:S(2)}, u32[]{:S(2)}) collective-permute-start(bf16[1024,2048]{1,0:T(8,128)(2,1)} %get-tuple-element.58), channel_id=1, source_target_pairs={{0,2},{1,5},{2,0},{3,7},{4,6},{5,1},{6,4},{7,3},{8,10},{9,13},{10,... | collective-permute-start | bytes 12582920 | tf_op jit(solution)/shard_map/ppermute | solution.py:42
  148.0 105.8 %collective-permute-start.12 = (bf16[1024,2048]{1,0:T(8,128)(2,1)}, bf16[1024,2048]{1,0:T(8,128)(2,1)}, u32[]{:S(2)}, u32[]{:S(2)}) collective-permute-start(bf16[1024,2048]{1,0:T(8,128)(2,1)} %dynamic-slice_bitcast_fusion.1), channel_id=1, source_target_pairs={{0,8},{1,9},{2,10},{3,11},{4,12},{5,13},{6,14},{7,15},{8,0},{9,1},... | collective-permute-start | bytes 12582920 | tf_op jit(solution)/shard_map/ppermute | solution.py:42
  164.6 97.9 %collective-permute-start.10 = (bf16[1024,2048]{1,0:T(8,128)(2,1)}, bf16[1024,2048]{1,0:T(8,128)(2,1)}, u32[]{:S(2)}, u32[]{:S(2)}) collective-permute-start(bf16[1024,2048]{1,0:T(8,128)(2,1)} %collective-permute-done.8.refs_0_), channel_id=1, source_target_pairs={{0,2},{1,5},{2,0},{3,7},{4,6},{5,1},{6,4},{7,3},{8,10},{9,13},{10,... | collective-permute-start | bytes 12582920 | tf_op jit(solution)/shard_map/ppermute | solution.py:42
  193.6 62.0 %collective-permute-start.3 = (bf16[512,2048]{1,0:T(8,128)(2,1)S(1)}, bf16[512,2048]{1,0:T(8,128)(2,1)}, u32[]{:S(2)}, u32[]{:S(2)}) collective-permute-start(bf16[512,2048]{1,0:T(8,128)(2,1)S(1)} %add_convert_fusion.2), channel_id=1, source_target_pairs={{0,4},{1,3},{2,6},{3,1},{4,0},{5,7},{6,2},{7,5},{8,12},{9,11},{10,... | collective-permute-start | bytes 6291464 | tf_op jit(solution)/shard_map/ppermute | solution.py:42
  253.9 71.5 %collective-permute-start.14 = (bf16[1024,2048]{1,0:T(8,128)(2,1)}, bf16[1024,2048]{1,0:T(8,128)(2,1)}, u32[]{:S(2)}, u32[]{:S(2)}) collective-permute-start(bf16[1024,2048]{1,0:T(8,128)(2,1)} %collective-permute-done.12.refs_0_.refs_4_), channel_id=1, source_target_pairs={{0,2},{1,5},{2,0},{3,7},{4,6},{5,1},{6,4},{7,3},{8,10},{9,13},{10,... | collective-permute-start | bytes 12582920 | tf_op jit(solution)/shard_map/ppermute | solution.py:42
  260.9 53.8 %copy-start = (bf16[512,2048]{1,0:T(8,128)(2,1)}, bf16[512,2048]{1,0:T(8,128)(2,1)S(1)}, u32[]{:S(2)}) copy-start(bf16[512,2048]{1,0:T(8,128)(2,1)S(1)} %fusion) | copy-start | bytes 6291460
  260.9 48.6 %collective-permute-start.4 = (bf16[512,2048]{1,0:T(8,128)(2,1)S(1)}, bf16[512,2048]{1,0:T(8,128)(2,1)}, u32[]{:S(2)}, u32[]{:S(2)}) collective-permute-start(bf16[512,2048]{1,0:T(8,128)(2,1)S(1)} %fusion), channel_id=1, source_target_pairs={{0,4},{1,3},{2,6},{3,1},{4,0},{5,7},{6,2},{7,5},{8,12},{9,11},{10,... | collective-permute-start | bytes 6291464 | tf_op jit(solution)/shard_map/ppermute | solution.py:42
  262.5 88.6 %collective-permute-start.9 = (bf16[1024,2048]{1,0:T(8,128)(2,1)}, bf16[1024,2048]{1,0:T(8,128)(2,1)}, u32[]{:S(2)}, u32[]{:S(2)}) collective-permute-start(bf16[1024,2048]{1,0:T(8,128)(2,1)} %collective-permute-done.8.refs_0_), channel_id=1, source_target_pairs={{0,1},{1,0},{2,3},{3,2},{4,5},{5,4},{6,7},{7,6},{8,9},{9,8},{10,11... | collective-permute-start | bytes 12582920 | tf_op jit(solution)/shard_map/ppermute | solution.py:42
  262.5 88.6 %collective-permute-start.11 = (bf16[1024,2048]{1,0:T(8,128)(2,1)}, bf16[1024,2048]{1,0:T(8,128)(2,1)}, u32[]{:S(2)}, u32[]{:S(2)}) collective-permute-start(bf16[1024,2048]{1,0:T(8,128)(2,1)} %collective-permute-done.10.refs_2_), channel_id=1, source_target_pairs={{0,1},{1,0},{2,3},{3,2},{4,5},{5,4},{6,7},{7,6},{8,9},{9,8},{10,11... | collective-permute-start | bytes 12582920 | tf_op jit(solution)/shard_map/ppermute | solution.py:42
  314.7 60.5 %collective-permute-start.5 = (bf16[1024,2048]{1,0:T(8,128)(2,1)}, bf16[1024,2048]{1,0:T(8,128)(2,1)}, u32[]{:S(2)}, u32[]{:S(2)}) collective-permute-start(bf16[1024,2048]{1,0:T(8,128)(2,1)} %maximum_select_fusion.refs_0_.refs_4_), channel_id=1, source_target_pairs={{0,2},{1,5},{2,0},{3,7},{4,6},{5,1},{6,4},{7,3},{8,10},{9,13},{10,... | collective-permute-start | bytes 12582920 | tf_op jit(solution)/shard_map/ppermute | solution.py:42
  315.1 60.2 %collective-permute-start.13 = (bf16[1024,2048]{1,0:T(8,128)(2,1)}, bf16[1024,2048]{1,0:T(8,128)(2,1)}, u32[]{:S(2)}, u32[]{:S(2)}) collective-permute-start(bf16[1024,2048]{1,0:T(8,128)(2,1)} %collective-permute-done.12.refs_0_.refs_4_), channel_id=1, source_target_pairs={{0,1},{1,0},{2,3},{3,2},{4,5},{5,4},{6,7},{7,6},{8,9},{9,8},{10,11... | collective-permute-start | bytes 12582920 | tf_op jit(solution)/shard_map/ppermute | solution.py:42
  325.4 68.7 %collective-permute-start.15 = (bf16[1024,2048]{1,0:T(8,128)(2,1)}, bf16[1024,2048]{1,0:T(8,128)(2,1)}, u32[]{:S(2)}, u32[]{:S(2)}) collective-permute-start(bf16[1024,2048]{1,0:T(8,128)(2,1)} %collective-permute-done.14.refs_0_.refs_6_), channel_id=1, source_target_pairs={{0,1},{1,0},{2,3},{3,2},{4,5},{5,4},{6,7},{7,6},{8,9},{9,8},{10,11... | collective-permute-start | bytes 12582920 | tf_op jit(solution)/shard_map/ppermute | solution.py:42
  374.7 94.6 %collective-permute-start.6 = (bf16[1024,2048]{1,0:T(8,128)(2,1)}, bf16[1024,2048]{1,0:T(8,128)(2,1)}, u32[]{:S(2)}, u32[]{:S(2)}) collective-permute-start(bf16[1024,2048]{1,0:T(8,128)(2,1)} %maximum_select_fusion.refs_0_.refs_4_), channel_id=1, source_target_pairs={{0,1},{1,0},{2,3},{3,2},{4,5},{5,4},{6,7},{7,6},{8,9},{9,8},{10,11... | collective-permute-start | bytes 12582920 | tf_op jit(solution)/shard_map/ppermute | solution.py:42
  375.2 94.1 %collective-permute-start.7 = (bf16[1024,2048]{1,0:T(8,128)(2,1)}, bf16[1024,2048]{1,0:T(8,128)(2,1)}, u32[]{:S(2)}, u32[]{:S(2)}) collective-permute-start(bf16[1024,2048]{1,0:T(8,128)(2,1)} %collective-permute-done.5.refs_1_.refs_5_), channel_id=1, source_target_pairs={{0,1},{1,0},{2,3},{3,2},{4,5},{5,4},{6,7},{7,6},{8,9},{9,8},{10,11... | collective-permute-start | bytes 12582920 | tf_op jit(solution)/shard_map/ppermute | solution.py:42
  527.6 46.6 %collective-permute-start.16 = (bf16[2,1024,2048]{2,1,0:T(8,128)(2,1)}, bf16[2,1024,2048]{2,1,0:T(8,128)(2,1)}, u32[]{:S(2)}, u32[]{:S(2)}) collective-permute-start(bf16[2,1024,2048]{2,1,0:T(8,128)(2,1)} %get-tuple-element.74.refs_6_.refs_7_), channel_id=1, source_target_pairs={{0,1},{1,0},{2,3},{3,2},{4,5},{5,4},{6,7},{7,6},{8,9},{9,8},{10,11... | collective-permute-start | bytes 25165832 | tf_op jit(solution)/shard_map/ppermute | solution.py:42
  528.1 93.8 %collective-permute-start.29 = (bf16[1024,2048]{1,0:T(8,128)(2,1)}, bf16[1024,2048]{1,0:T(8,128)(2,1)}, u32[]{:S(2)}, u32[]{:S(2)}) collective-permute-start(bf16[1024,2048]{1,0:T(8,128)(2,1)} %get-tuple-element.101), channel_id=1, source_target_pairs={{0,8},{1,9},{2,10},{3,11},{4,12},{5,13},{6,14},{7,15},{8,0},{9,1},... | collective-permute-start | bytes 12582920 | tf_op jit(solution)/shard_map/ppermute | solution.py:42
  529.6 181.2 %collective-permute-start.25 = (bf16[1024,2048]{1,0:T(8,128)(2,1)}, bf16[1024,2048]{1,0:T(8,128)(2,1)}, u32[]{:S(2)}, u32[]{:S(2)}) collective-permute-start(bf16[1024,2048]{1,0:T(8,128)(2,1)} %maximum_select_fusion.refs_0_.refs_4_), channel_id=1, source_target_pairs={{0,8},{1,9},{2,10},{3,11},{4,12},{5,13},{6,14},{7,15},{8,0},{9,1},... | collective-permute-start | bytes 12582920 | tf_op jit(solution)/shard_map/ppermute | solution.py:42
  617.5 164.6 %copy-start.1 = (bf16[512,2048]{1,0:T(8,128)(2,1)S(1)}, bf16[512,2048]{1,0:T(8,128)(2,1)}, u32[]{:S(2)}) copy-start(bf16[512,2048]{1,0:T(8,128)(2,1)} %copy-done) | copy-start | bytes 6291460
  617.5 164.6 %copy-start.2 = (bf16[1024,2048]{1,0:T(8,128)(2,1)S(1)}, bf16[1024,2048]{1,0:T(8,128)(2,1)}, u32[]{:S(2)}) copy-start(bf16[1024,2048]{1,0:T(8,128)(2,1)} %get-tuple-element.79) | copy-start | bytes 12582916
  617.5 94.7 %collective-permute-start.17 = (bf16[1024,2048]{1,0:T(8,128)(2,1)}, bf16[1024,2048]{1,0:T(8,128)(2,1)S(1)}, u32[]{:S(2)}, u32[]{:S(2)}) collective-permute-start(bf16[1024,2048]{1,0:T(8,128)(2,1)} %get-tuple-element.80), channel_id=1, source_target_pairs={{0,2},{1,5},{2,0},{3,7},{4,6},{5,1},{6,4},{7,3},{8,10},{9,13},{10,... | collective-permute-start | bytes 12582920 | tf_op jit(solution)/shard_map/ppermute | solution.py:42
  621.8 94.4 %collective-permute-start.31 = (bf16[1024,2048]{1,0:T(8,128)(2,1)}, bf16[1024,2048]{1,0:T(8,128)(2,1)}, u32[]{:S(2)}, u32[]{:S(2)}) collective-permute-start(bf16[1024,2048]{1,0:T(8,128)(2,1)} %collective-permute-done.29.refs_0_), channel_id=1, source_target_pairs={{0,2},{1,5},{2,0},{3,7},{4,6},{5,1},{6,4},{7,3},{8,10},{9,13},{10,... | collective-permute-start | bytes 12582920 | tf_op jit(solution)/shard_map/ppermute | solution.py:42
  710.8 71.3 %collective-permute-start.27 = (bf16[1024,2048]{1,0:T(8,128)(2,1)}, bf16[1024,2048]{1,0:T(8,128)(2,1)}, u32[]{:S(2)}, u32[]{:S(2)}) collective-permute-start(bf16[1024,2048]{1,0:T(8,128)(2,1)} %collective-permute-done.25.refs_0_.refs_4_), channel_id=1, source_target_pairs={{0,2},{1,5},{2,0},{3,7},{4,6},{5,1},{6,4},{7,3},{8,10},{9,13},{10,... | collective-permute-start | bytes 12582920 | tf_op jit(solution)/shard_map/ppermute | solution.py:42
  714.7 67.4 %collective-permute-start.18 = (bf16[512,2048]{1,0:T(8,128)(2,1)S(1)}, bf16[512,2048]{1,0:T(8,128)(2,1)S(1)}, u32[]{:S(2)}, u32[]{:S(2)}) collective-permute-start(bf16[512,2048]{1,0:T(8,128)(2,1)S(1)} %add_convert_fusion.1), channel_id=1, source_target_pairs={{0,4},{1,3},{2,6},{3,1},{4,0},{5,7},{6,2},{7,5},{8,12},{9,11},{10,... | collective-permute-start | bytes 6291464 | tf_op jit(solution)/shard_map/ppermute | solution.py:42
  716.2 120.6 %collective-permute-start.30 = (bf16[1024,2048]{1,0:T(8,128)(2,1)}, bf16[1024,2048]{1,0:T(8,128)(2,1)}, u32[]{:S(2)}, u32[]{:S(2)}) collective-permute-start(bf16[1024,2048]{1,0:T(8,128)(2,1)} %collective-permute-done.29.refs_0_), channel_id=1, source_target_pairs={{0,1},{1,0},{2,3},{3,2},{4,5},{5,4},{6,7},{7,6},{8,9},{9,8},{10,11... | collective-permute-start | bytes 12582920 | tf_op jit(solution)/shard_map/ppermute | solution.py:42
  716.2 121.1 %collective-permute-start.32 = (bf16[1024,2048]{1,0:T(8,128)(2,1)}, bf16[1024,2048]{1,0:T(8,128)(2,1)}, u32[]{:S(2)}, u32[]{:S(2)}) collective-permute-start(bf16[1024,2048]{1,0:T(8,128)(2,1)} %collective-permute-done.31.refs_2_), channel_id=1, source_target_pairs={{0,1},{1,0},{2,3},{3,2},{4,5},{5,4},{6,7},{7,6},{8,9},{9,8},{10,11... | collective-permute-start | bytes 12582920 | tf_op jit(solution)/shard_map/ppermute | solution.py:42
  716.7 165.4 %collective-permute-start.26 = (bf16[1024,2048]{1,0:T(8,128)(2,1)}, bf16[1024,2048]{1,0:T(8,128)(2,1)}, u32[]{:S(2)}, u32[]{:S(2)}) collective-permute-start(bf16[1024,2048]{1,0:T(8,128)(2,1)} %collective-permute-done.25.refs_0_.refs_4_), channel_id=1, source_target_pairs={{0,1},{1,0},{2,3},{3,2},{4,5},{5,4},{6,7},{7,6},{8,9},{9,8},{10,11... | collective-permute-start | bytes 12582920 | tf_op jit(solution)/shard_map/ppermute | solution.py:42
  782.1 100.1 %collective-permute-start.28 = (bf16[1024,2048]{1,0:T(8,128)(2,1)}, bf16[1024,2048]{1,0:T(8,128)(2,1)}, u32[]{:S(2)}, u32[]{:S(2)}) collective-permute-start(bf16[1024,2048]{1,0:T(8,128)(2,1)} %collective-permute-done.27.refs_2_.refs_6_), channel_id=1, source_target_pairs={{0,1},{1,0},{2,3},{3,2},{4,5},{5,4},{6,7},{7,6},{8,9},{9,8},{10,11... | collective-permute-start | bytes 12582920 | tf_op jit(solution)/shard_map/ppermute | solution.py:42
  784.0 45.7 %collective-permute-start.19 = (bf16[512,2048]{1,0:T(8,128)(2,1)S(1)}, bf16[512,2048]{1,0:T(8,128)(2,1)}, u32[]{:S(2)}, u32[]{:S(2)}) collective-permute-start(bf16[512,2048]{1,0:T(8,128)(2,1)S(1)} %add_convert_fusion), channel_id=1, source_target_pairs={{0,4},{1,3},{2,6},{3,1},{4,0},{5,7},{6,2},{7,5},{8,12},{9,11},{10,... | collective-permute-start | bytes 6291464 | tf_op jit(solution)/shard_map/ppermute | solution.py:42
  829.7 201.4 %collective-permute-start.24 = (f32[2048,1024]{1,0:T(8,128)}, f32[2048,1024]{1,0:T(8,128)}, u32[]{:S(2)}, u32[]{:S(2)}) collective-permute-start(f32[2048,1024]{1,0:T(8,128)} %get-tuple-element.82), channel_id=1, source_target_pairs={{0,8},{1,9},{2,10},{3,11},{4,12},{5,13},{6,14},{7,15},{8,0},{9,1},... | collective-permute-start | bytes 25165832 | tf_op jit(solution)/shard_map/ppermute | solution.py:42
  836.8 355.5 %collective-permute-start.23 = (f32[1024,2048]{1,0:T(8,128)}, f32[1024,2048]{1,0:T(8,128)}, u32[]{:S(2)}, u32[]{:S(2)}) collective-permute-start(f32[1024,2048]{1,0:T(8,128)} %get-tuple-element.81), channel_id=1, source_target_pairs={{0,8},{1,9},{2,10},{3,11},{4,12},{5,13},{6,14},{7,15},{8,0},{9,1},... | collective-permute-start | bytes 25165832 | tf_op jit(solution)/shard_map/ppermute | solution.py:42
  837.3 102.4 %collective-permute-start.20 = (bf16[1024,2048]{1,0:T(8,128)(2,1)}, bf16[1024,2048]{1,0:T(8,128)(2,1)}, u32[]{:S(2)}, u32[]{:S(2)}) collective-permute-start(bf16[1024,2048]{1,0:T(8,128)(2,1)} %maximum_select_fusion.1.refs_0_), channel_id=1, source_target_pairs={{0,2},{1,5},{2,0},{3,7},{4,6},{5,1},{6,4},{7,3},{8,10},{9,13},{10,... | collective-permute-start | bytes 12582920 | tf_op jit(solution)/shard_map/ppermute | solution.py:42
  939.7 252.6 %collective-permute-start.21 = (bf16[1024,2048]{1,0:T(8,128)(2,1)}, bf16[1024,2048]{1,0:T(8,128)(2,1)}, u32[]{:S(2)}, u32[]{:S(2)}) collective-permute-start(bf16[1024,2048]{1,0:T(8,128)(2,1)} %maximum_select_fusion.1.refs_0_), channel_id=1, source_target_pairs={{0,1},{1,0},{2,3},{3,2},{4,5},{5,4},{6,7},{7,6},{8,9},{9,8},{10,11... | collective-permute-start | bytes 12582920 | tf_op jit(solution)/shard_map/ppermute | solution.py:42
  939.8 252.6 %collective-permute-start.22 = (bf16[1024,2048]{1,0:T(8,128)(2,1)}, bf16[1024,2048]{1,0:T(8,128)(2,1)}, u32[]{:S(2)}, u32[]{:S(2)}) collective-permute-start(bf16[1024,2048]{1,0:T(8,128)(2,1)} %collective-permute-done.20.refs_1_), channel_id=1, source_target_pairs={{0,1},{1,0},{2,3},{3,2},{4,5},{5,4},{6,7},{7,6},{8,9},{9,8},{10,11... | collective-permute-start | bytes 12582920 | tf_op jit(solution)/shard_map/ppermute | solution.py:42

commit v2 on v1

--- a/solution.py
+++ b/solution.py
@@ -109,7 +109,7 @@
     return jnp.concatenate([r[...] for r in refs], axis=axis)
 
 
-def hidden_grad(order, token, grad, hidden, w_down, layer, half):
+def hidden_grad(order, token, grad, hidden, w_down, layer, half, keep=False, put=None):
     n = len(grad)
     cols = BN if half else F
     groups = n // 2
@@ -126,6 +126,10 @@
         d = (act * slope).reshape(n, BM // n, BN).astype(BF16)
         for k in range(groups):
             outs[1 + k][...] = d[2 * k:2 * k + 2]
+        if keep:
+            outs[1 + groups][...] = ins[0][...]
+        if put is not None:
+            outs[1 + groups][...] = ins[2 * n + 1][...]
 
     ins = [p.spec(BM // n, D, lambda j, i, o: (i, 0)) for p in grad]
     ins += [p.spec(BM // n, BN, lambda j, i, o: (i, j)) for p in hidden]
@@ -134,7 +138,13 @@
     def out(m):
         return (jax.ShapeDtypeStruct((m, PIECE, cols), BF16), pl.BlockSpec((m, BM // n, BN), lambda j, i, o: (0, i, j)))
 
-    *res, tok = call(body, (cols // BN, n * PIECE // BM), ins, [out(n)] + [out(2)] * groups, 2 * n * PIECE * D * cols, order, token)
+    kept = [(jax.ShapeDtypeStruct((PIECE, D), BF16), pl.BlockSpec((BM // n, D), lambda j, i, o: (i, 0)))] if keep else []
+    aliases = None
+    if put is not None:
+        ins += [(put[0], pl.BlockSpec((64, D), lambda j, i, o: (8 * j + i, 0))), (put[1], ANY_SPEC)]
+        kept = [(STACK, pl.BlockSpec((None, 64, D), lambda j, i, o: (1, 16 * o[THEIRS] + 8 * j + i, 0)))]
+        aliases = {2 * n + 2: 1 + groups}
+    *res, tok = call(body, (cols // BN, n * PIECE // BM), ins, [out(n)] + [out(2)] * groups + kept, 2 * n * PIECE * D * cols, order, token, aliases)
     return res[0], res[1:], tok
 
 
@@ -191,6 +201,31 @@
     tile = pl.BlockSpec((None, BN, BN), lambda i, j, o: (0, i, j))
     step = (2, lambda k, o: k)
     return weight_grad(order, token, left, right, step, step, BN, [(total, tile if add else ANY_SPEC)], [(STACK, tile)], add, {0: 0})
+
+
+def weight_last(order, token, left, right, total, pieces):
+    n, bn = len(left), 512
+    tile = pl.BlockSpec((None, BN, bn), lambda i, j, o: (0, i, j))
+
+    def body(ins, outs):
+        acc = lax.dot_general(join(ins[:n]), join(ins[n:2 * n]), TN, preferred_element_type=jnp.float32)
+        outs[0][...] = acc + ins[2 * n][...]
+        step = 4 * pl.program_id(0) + pl.program_id(1)
+        for k in range(3):
+            @pl.when(step // 2 == k)
+            def _(k=k):
+                outs[1][...] = ins[2 * n + 1 + k][...]
+
+    def row(i, j):
+        return jnp.minimum(4 * i + j, 5)
+
+    ins = [p.spec(PIECE, BN, lambda i, j, o: (0, i)) for p in left]
+    ins += [p.spec(PIECE, bn, lambda i, j, o: (0, j)) for p in right]
+    ins.append((total, tile))
+    ins += [p.spec(BM, D, lambda i, j, o, k=k: (jnp.clip(4 * i + j - 2 * k, 0, 1), 0)) for k, p in enumerate(pieces)]
+    outs = [(STACK, tile),
+            (jax.ShapeDtypeStruct((4, PIECE, D), BF16), pl.BlockSpec((None, BM, D), lambda i, j, o: (o[row(i, j) // 2], row(i, j) % 2, 0)))]
+    return call(body, (2, 4), ins, outs, 2 * n * PIECE * 2048 * 2048, order, token, {2 * n: 0})
 
 
 def weight_half(order, token, left, right, down, prev):
@@ -210,23 +245,15 @@
     return weight_grad(order, token, left, right, *cols, bn, [] if prev is None else [(prev, tile)], outs, prev is not None, None)
 
 
-def finish(order, token, pieces, down_in, up_in, down, up):
-    def body(ins, outs):
-        i = pl.program_id(0)
-        for k in range(4):
-            @pl.when(i // 2 == k)
-            def _(k=k):
-                outs[0][...] = ins[k][...]
-        outs[1][...] = ins[4][...]
-        outs[2][...] = ins[5][...]
-
-    ins = [p.spec(BM, D, lambda i, o, k=k: (jnp.clip(i - 2 * k, 0, 1), 0)) for k, p in enumerate(pieces)]
-    ins += [(down_in, pl.BlockSpec((128, D), lambda i, o: (i, 0))), (up_in, pl.BlockSpec((256, BN), lambda i, o: (i, 0)))]
-    ins += [(down, ANY_SPEC), (up, ANY_SPEC)]
-    outs = [(jax.ShapeDtypeStruct((4, PIECE, D), BF16), pl.BlockSpec((None, BM, D), lambda i, o: (o[i // 2], i % 2, 0))),
-            (STACK, pl.BlockSpec((None, 128, D), lambda i, o: (1, 8 * o[THEIRS] + i, 0))),
-            (STACK, pl.BlockSpec((None, 256, BN), lambda i, o: (1, i, o[THEIRS])))]
-    return call(body, (8,), ins, outs, 1000, order, token, {6: 1, 7: 2})
+def finish(order, token, last, grad, up_in, up):
+    def body(ins, outs):
+        outs[0][...] = ins[0][...]
+        outs[1][...] = ins[1][...]
+
+    ins = [last.spec(256, D, lambda i, o: (i, 0)), (up_in, pl.BlockSpec((512, BN), lambda i, o: (i, 0))), (grad, ANY_SPEC), (up, ANY_SPEC)]
+    outs = [(jax.ShapeDtypeStruct((4, PIECE, D), BF16), pl.BlockSpec((None, 256, D), lambda i, o: (o[3], i, 0))),
+            (STACK, pl.BlockSpec((None, 512, BN), lambda i, o: (1, i, o[THEIRS])))]
+    return call(body, (4,), ins, outs, 1000, order, token, {2: 0, 3: 1})
 
 
 def f32(v):
@@ -247,36 +274,36 @@
         def both_halves(mine, other):
             return jnp.where(sub == 0, jnp.concatenate([mine, other]), jnp.concatenate([other, mine]))
 
-        def own_block(arr, *lead):
-            idx = tuple(lead) + (order[0], 0, 0)
-            return lax.dynamic_slice(arr, idx, (1,) * (len(lead) + 1) + (PIECE, D)).reshape(PIECE, D)
+        def own_block(arr, lead, after):
+            idx = (lead, order[0] + after[0, 0].astype(jnp.int32), 0, 0)
+            return lax.dynamic_slice(arr, idx, (1, 1, PIECE, D)).reshape(PIECE, D)
 
         def summed(p02, near, which):
             return f32(my_half(p02, which)) + f32(my_half(near, which))
 
-        x1z = send(own_block(x_nat, 1), PERM_Z)
+        x1z = send(own_block(x_nat, 1, tok), PERM_Z)
         w_core = send(w_up, PERM_C)
-        g2mine = own_block(g_nat)
+        g2 = natural(g_nat)
+        a1, (dm, do, g2mine), tok = hidden_grad(order, tok, g2, natural(h_nat, 1), w_down, 1, False, True)
         g2z = send(g2mine, PERM_Z)
-        g2 = natural(g_nat)
-        a1, (dm, do), tok = hidden_grad(order, tok, g2, natural(h_nat, 1), w_down, 1, False)
         dc = send(do, PERM_C)
         down_h, tok = weight_half(order, tok, parts(a1), g2, True, None)
         x1c0 = send(x1z, PERM_C)
         x1s = send(x1z, PERM_S1)
         p02, p13, tok = back_term(order, tok, dm, dc, w_up, w_core, 1)
         near = send(p13, PERM_S1)
-        up_h, tok = weight_half(order, tok, natural(x_nat, 1), parts(dm) + parts(do), False, None)
         x1c1 = send(x1s, PERM_C)
-        x0z = send(own_block(x_nat, 0), PERM_Z)
         hp, tok = hidden_again(order, tok, whole(x1z, x1c0, x1s, x1c1), w_up, 1, True)
+        x0z = send(own_block(x_nat, 0, tok), PERM_Z)
         g2c0 = send(g2z, PERM_C)
         g2s = send(g2z, PERM_S1)
         far = send(summed(p02, near, 1 - sub).astype(BF16), PERM_S2)
         apa, (dpa,), tok = hidden_grad(order, tok, whole(g2z, g2c0), [Piece(hp, 0), Piece(hp, 1)], w_down, 1, True)
-        g2c1 = send(g2s, PERM_C)
+        up_h, tok = weight_half(order, tok, natural(x_nat, 1), parts(dm) + parts(do), False, None)
         g1m0 = (f32(my_half(g2mine, sub)) + (summed(p02, near, sub) + f32(far))).astype(BF16)
         g1m2 = send(g1m0, PERM_S2)
+        g2s, _ = lax.optimization_barrier((g2s, g1m0))
+        g2c1 = send(g2s, PERM_C)
         apb, (dpb,), tok = hidden_grad(order, tok, whole(g2s, g2c1), [Piece(hp, 2), Piece(hp, 3)], w_down, 1, True)
         g1mine = both_halves(g1m0, g1m2)
         g1s = send(g1mine, PERM_S1)
@@ -306,14 +333,14 @@
         g0m0 = (f32(g1m0) + (summed(p02, near, sub) + f32(far))).astype(BF16)
         g0m2 = send(g0m0, PERM_S2)
         g1p = whole(g1zp, g1cp0, g1sp, g1cp1)
-        ap, (dma, dmb), tok = hidden_grad(order, tok, g1p, parts(hp), w_down, 0, False)
+        ap, (dma, dmb, down), tok = hidden_grad(order, tok, g1p, parts(hp), w_down, 0, False, put=(down_in, down))
         g0mine = both_halves(g0m0, g0m2)
         g0s = send(g0mine, PERM_S1)
         g0c0 = send(g0mine, PERM_C)
-        down, tok = weight_full(order, tok, parts(ap), g1p, down, True)
+        up, tok = weight_full(order, tok, whole(x0z, x0c0, x0s, x0c1), parts(dma) + parts(dmb), up, True)
         g0c1 = send(g0s, PERM_C)
-        up, tok = weight_full(order, tok, whole(x0z, x0c0, x0s, x0c1), parts(dma) + parts(dmb), up, True)
-        grad_in, down, up, tok = finish(order, tok, whole(g0mine, g0s, g0c0, g0c1), down_in, up_in, down, up)
+        down, grad_in, tok = weight_last(order, tok, parts(ap), g1p, down, whole(g0mine, g0s, g0c0))
+        grad_in, up, tok = finish(order, tok, Piece(g0c1), grad_in, up_in, up)
         return grad_in.reshape(1, 4 * PIECE, D), up, down
 
     body = jax.shard_map(

time: 1230 us -> 1190 us (0.967)
  waiting for transfers between devices: 473 us -> 445 us
    ppermute x33, waiting for transfers between devices: 473 us -> 445 us  [send(): return lax.ppermute(value, AXES, pairs)]
  transfers between devices with their start and end apart: 33 -> 33, of which waited for: 9 -> 12; matrix products, arithmetic and copies ran while one was open for 3% -> 3% of each run, Pallas kernels for 49% -> 47%
where the time goes in v2:
time: 1190 us; the launch traced here: 1180 us
  Pallas kernels  671 us (56%)
  waiting for transfers between devices  445 us (37%)
  starting transfers between devices  27.3 us (2%)
  other arithmetic  24.4 us (2%)
    pallas_call x18, Pallas kernels, call(): pl.pallas_call(wrapped, grid_spec=pltpu.PrefetchScalarGridSpec(num_scalar...  671 us
    ppermute x33, waiting for transfers between devices, send(): return lax.ppermute(value, AXES, pairs)  445 us
    ppermute x33, starting transfers between devices, send(): return lax.ppermute(value, AXES, pairs)  27.3 us
  transfers between devices with their start and end apart: 33, of which 12 were waited for; matrix products, arithmetic and copies ran while one was open for 3% of the time, Pallas kernels for 47%

profile of v2, /device:TPU:0, one launch (start us, length us, event | category | flops | bytes accessed | tf_op | source)
XLA Modules:
  0.0 1181.2 jit_solution(10641064903087210799)
XLA Ops:
  0.6 0.8 collective-permute-start.1
  1.4 0.6 stack.27.order_ref
  2.0 0.6 broadcast_in_dim.3.refs_9_
  2.6 59.8 %shard_map.76 = (bf16[4,1024,2048]{2,1,0:T(8,128)(2,1)}, bf16[2,1024,2048]{2,1,0:T(8,128)(2,1)}, bf16[2,1024,2048]{2,1,0:T(8,128)(2,1)}, bf16[1024,2048]{1,0:T(8,128)(2,1)}, f32[8,128]{1,0:T(8,128)}) custom-call(s32[6]{0:T(128)} %stack.27.order_ref, bf16[4,1024,2048]{2,1,0:T(8,128)(2,1)} %bitcast.33, bf16[4,1024,2048]{2,1,0:T(8,128)(2,1)} %bitcast.34, ...), custom_call_target="tpu_custom_call" | custom-call | flops 34359738368 | bytes 60000000 | tf_op jit(solution)/shard_map/pallas_call | solution.py:68
  62.6 4.8 dynamic-slice_bitcast_fusion.1
  67.3 3.0 collective-permute-start.8
  70.3 25.5 %shard_map.77 = (f32[1024,2048]{1,0:T(8,128)}, f32[8,128]{1,0:T(8,128)}) custom-call(s32[6]{0:T(128)} %stack.27.order_ref, bf16[4,1024,2048]{2,1,0:T(8,128)(2,1)} %get-tuple-element.58.refs_0_.refs_1_.refs_2_.refs_3_, bf16[4,1024,2048]{2,1,0:T(8,128)(2,1)} %get-tuple-element.58.refs_0_.refs_1_.refs_2_.refs_3_, ...), custom_call_target="tpu_custom_call" | custom-call | flops 17179869184 | bytes 60000000 | tf_op jit(solution)/shard_map/pallas_call | solution.py:68
  95.8 43.6 %shard_map.78 = (bf16[1024,2048]{1,0:T(8,128)(2,1)}, bf16[1024,2048]{1,0:T(8,128)(2,1)}, f32[8,128]{1,0:T(8,128)}) custom-call(s32[6]{0:T(128)} %stack.27.order_ref, bf16[2,1024,2048]{2,1,0:T(8,128)(2,1)} %get-tuple-element.56.refs_0_.refs_1_.refs_4_.refs_5_, bf16[2,1024,2048]{2,1,0:T(8,128)(2,1)} %get-tuple-element.56.refs_0_.refs_1_.refs_4_.refs_5_, ...), custom_call_target="tpu_custom_call" | custom-call | flops 34359738368 | bytes 60000000 | tf_op jit(solution)/shard_map/pallas_call | solution.py:68
  139.4 1.5 collective-permute-start.2
  141.4 20.7 %collective-permute-done.8.refs_0_ = bf16[1024,2048]{1,0:T(8,128)(2,1)} collective-permute-done((bf16[1024,2048]{1,0:T(8,128)(2,1)}, bf16[1024,2048]{1,0:T(8,128)(2,1)}, u32[]{:S(2)}, u32[]{:S(2)}) %collective-permute-start.8) | collective-permute-done | bytes 4194336 | tf_op jit(solution)/shard_map/ppermute | solution.py:42
  162.1 1.9 collective-permute-start.10
  164.0 24.3 %collective-permute-done.2 = bf16[1024,2048]{1,0:T(8,128)(2,1)} collective-permute-done((bf16[1024,2048]{1,0:T(8,128)(2,1)}, bf16[1024,2048]{1,0:T(8,128)(2,1)}, u32[]{:S(2)}, u32[]{:S(2)}) %collective-permute-start.2) | collective-permute-done | bytes 4194336 | tf_op jit(solution)/shard_map/ppermute | solution.py:42
  188.3 3.0 add_convert_fusion.3
  191.3 1.6 collective-permute-start.3
  192.8 58.5 %collective-permute-done.12.refs_0_.refs_4_ = bf16[1024,2048]{1,0:T(8,128)(2,1)} collective-permute-done((bf16[1024,2048]{1,0:T(8,128)(2,1)}, bf16[1024,2048]{1,0:T(8,128)(2,1)}, u32[]{:S(2)}, u32[]{:S(2)}) %collective-permute-start.12) | collective-permute-done | bytes 4194336 | tf_op jit(solution)/shard_map/ppermute | solution.py:42
  251.3 1.7 collective-permute-start.14
  253.0 5.2 add_convert_fusion.2
  258.3 1.6 collective-permute-start.4
  259.8 0.5 collective-permute-start.11
  260.3 46.6 %collective-permute-done.4 = bf16[512,2048]{1,0:T(8,128)(2,1)} collective-permute-done((bf16[512,2048]{1,0:T(8,128)(2,1)S(1)}, bf16[512,2048]{1,0:T(8,128)(2,1)}, u32[]{:S(2)}, u32[]{:S(2)}) %collective-permute-start.4) | collective-permute-done | bytes 2097184 | tf_op jit(solution)/shard_map/ppermute | solution.py:42
  306.9 5.2 maximum_select_fusion.refs_0_.refs_4_
  312.5 10.6 collective-permute-done.14.refs_0_.refs_6_
  323.1 23.6 %shard_map.79 = (bf16[4,1024,1024]{2,1,0:T(8,128)(2,1)}, f32[8,128]{1,0:T(8,128)}) custom-call(s32[6]{0:T(128)} %stack.27.order_ref, bf16[1024,2048]{1,0:T(8,128)(2,1)} %collective-permute-done.8.refs_0_, bf16[1024,2048]{1,0:T(8,128)(2,1)} %collective-permute-done.9.refs_1_, bf16[1024,2048]{1,0:T(8,128)(2,1)} %collective-permute-done.10.refs_2_, ...), custom_call_target="tpu_custom_call" | custom-call | flops 17179869184 | bytes 60000000 | tf_op jit(solution)/shard_map/pallas_call | solution.py:68
  346.7 18.2 %shard_map.80 = (bf16[2,1024,1024]{2,1,0:T(8,128)(2,1)}, bf16[2,1024,1024]{2,1,0:T(8,128)(2,1)}, f32[8,128]{1,0:T(8,128)}) custom-call(s32[6]{0:T(128)} %stack.27.order_ref, bf16[1024,2048]{1,0:T(8,128)(2,1)} %collective-permute-done.12.refs_0_.refs_4_, bf16[1024,2048]{1,0:T(8,128)(2,1)} %collective-permute-done.13.refs_1_.refs_5_, ...), custom_call_target="tpu_custom_call" | custom-call | flops 8589934592 | bytes 60000000 | tf_op jit(solution)/shard_map/pallas_call | solution.py:68
  364.9 0.5 collective-permute-start.6
  365.4 2.6 collective-permute-done.5.refs_1_.refs_5_
  368.0 25.9 %shard_map.81 = (f32[2048,1024]{1,0:T(8,128)}, f32[8,128]{1,0:T(8,128)}) custom-call(s32[6]{0:T(128)} %stack.27.order_ref, bf16[2,4,1024,2048]{3,2,1,0:T(8,128)(2,1)} %bitcast.16, bf16[2,4,1024,2048]{3,2,1,0:T(8,128)(2,1)} %bitcast.17, bf16[2,4,1024,2048]{3,2,1,0:T(8,128)(2,1)} %bitcast.18, bf16[2,4,1024,2048]{3,2,1,0:T(8,128)(2,1)} %bitcast.19, ...), custom_call_target="tpu_custom_call" | custom-call | flops 17179869184 | bytes 60000000 | tf_op jit(solution)/shard_map/pallas_call | solution.py:68
  394.0 18.2 %shard_map.82 = (bf16[2,1024,1024]{2,1,0:T(8,128)(2,1)}, bf16[2,1024,1024]{2,1,0:T(8,128)(2,1)}, f32[8,128]{1,0:T(8,128)}) custom-call(s32[6]{0:T(128)} %stack.27.order_ref, bf16[1024,2048]{1,0:T(8,128)(2,1)} %collective-permute-done.14.refs_0_.refs_6_, bf16[1024,2048]{1,0:T(8,128)(2,1)} %collective-permute-done.15.refs_1_.refs_7_, ...), custom_call_target="tpu_custom_call" | custom-call | flops 8589934592 | bytes 60000000 | tf_op jit(solution)/shard_map/pallas_call | solution.py:68
  412.2 26.9 %shard_map.83 = (f32[1024,2048]{1,0:T(8,128)}, f32[2,2048,2048]{2,1,0:T(8,128)}, f32[8,128]{1,0:T(8,128)}) custom-call(s32[6]{0:T(128)} %stack.27.order_ref, bf16[2,1024,1024]{2,1,0:T(8,128)(2,1)} %get-tuple-element.72.refs_0_.refs_1_, bf16[2,1024,1024]{2,1,0:T(8,128)(2,1)} %get-tuple-element.72.refs_0_.refs_1_, ...), custom_call_target="tpu_custom_call" | custom-call | flops 17179869184 | bytes 60000000 | tf_op jit(solution)/shard_map/pallas_call | solution.py:68
  439.1 30.1 %shard_map.84 = (f32[2048,1024]{1,0:T(8,128)}, f32[2,2048,2048]{2,1,0:T(8,128)}, f32[8,128]{1,0:T(8,128)}) custom-call(s32[6]{0:T(128)} %stack.27.order_ref, bf16[1024,2048]{1,0:T(8,128)(2,1)} %collective-permute-done.8.refs_0_, bf16[1024,2048]{1,0:T(8,128)(2,1)} %collective-permute-done.9.refs_1_, bf16[1024,2048]{1,0:T(8,128)(2,1)} %collective-permute-done.10.refs_2_, ...), custom_call_target="tpu_custom_call" | custom-call | flops 17179869184 | bytes 60000000 | tf_op jit(solution)/shard_map/pallas_call | solution.py:68
  469.3 58.2 %shard_map.85 = (bf16[4,1024,2048]{2,1,0:T(8,128)(2,1)}, bf16[2,1024,2048]{2,1,0:T(8,128)(2,1)}, bf16[2,1024,2048]{2,1,0:T(8,128)(2,1)}, f32[8,128]{1,0:T(8,128)}) custom-call(s32[6]{0:T(128)} %stack.27.order_ref, bf16[1024,2048]{1,0:T(8,128)(2,1)} %maximum_select_fusion.refs_0_.refs_4_, bf16[1024,2048]{1,0:T(8,128)(2,1)} %collective-permute-done.5.refs_1_.refs_5_, ...), custom_call_target="tpu_custom_call" | custom-call | flops 34359738368 | bytes 60000000 | tf_op jit(solution)/shard_map/pallas_call | solution.py:68
  527.4 0.5 collective-permute-start.16
  528.0 44.1 %shard_map.86 = (f32[2,2048,2048]{2,1,0:T(8,128)}, f32[8,128]{1,0:T(8,128)}) custom-call(s32[6]{0:T(128)} %stack.27.order_ref, bf16[4,1024,2048]{2,1,0:T(8,128)(2,1)} %get-tuple-element.80.refs_0_.refs_1_.refs_2_.refs_3_, bf16[4,1024,2048]{2,1,0:T(8,128)(2,1)} %get-tuple-element.80.refs_0_.refs_1_.refs_2_.refs_3_, ...), custom_call_target="tpu_custom_call", output_to_operand_aliasing={{0}: (9, {})} | custom-call | flops 34359738368 | bytes 60000000 | tf_op jit(solution)/shard_map/pallas_call | solution.py:68
  572.1 43.6 %shard_map.87 = (bf16[1024,2048]{1,0:T(8,128)(2,1)}, bf16[1024,2048]{1,0:T(8,128)(2,1)}, f32[8,128]{1,0:T(8,128)}) custom-call(s32[6]{0:T(128)} %stack.27.order_ref, bf16[2,1024,2048]{2,1,0:T(8,128)(2,1)} %get-tuple-element.78.refs_0_.refs_1_.refs_4_.refs_5_, bf16[2,1024,2048]{2,1,0:T(8,128)(2,1)} %get-tuple-element.78.refs_0_.refs_1_.refs_4_.refs_5_, ...), custom_call_target="tpu_custom_call" | custom-call | flops 34359738368 | bytes 60000000 | tf_op jit(solution)/shard_map/pallas_call | solution.py:68
  615.6 1.5 collective-permute-start.17
  617.1 1.2 slice.3
  619.0 2.7 dynamic-slice_bitcast_fusion
  621.7 1.3 collective-permute-start.27
  623.0 0.8 collective-permute-start.23
  623.7 40.7 %collective-permute-done.17 = bf16[1024,2048]{1,0:T(8,128)(2,1)} collective-permute-done((bf16[1024,2048]{1,0:T(8,128)(2,1)}, bf16[1024,2048]{1,0:T(8,128)(2,1)}, u32[]{:S(2)}, u32[]{:S(2)}) %collective-permute-start.17) | collective-permute-done | bytes 4194336 | tf_op jit(solution)/shard_map/ppermute | solution.py:42
  664.4 2.4 add_convert_fusion.1
  666.8 1.6 collective-permute-start.18
  668.4 46.9 %collective-permute-done.27.refs_0_ = bf16[1024,2048]{1,0:T(8,128)(2,1)} collective-permute-done((bf16[1024,2048]{1,0:T(8,128)(2,1)S(1)}, bf16[1024,2048]{1,0:T(8,128)(2,1)}, u32[]{:S(2)}, u32[]{:S(2)}) %collective-permute-start.27) | collective-permute-done | bytes 4194336 | tf_op jit(solution)/shard_map/ppermute | solution.py:42
  715.3 0.5 collective-permute-start.29
  715.8 88.2 %collective-permute-done.23.refs_0_.refs_4_ = bf16[1024,2048]{1,0:T(8,128)(2,1)} collective-permute-done((bf16[1024,2048]{1,0:T(8,128)(2,1)}, bf16[1024,2048]{1,0:T(8,128)(2,1)}, u32[]{:S(2)}, u32[]{:S(2)}) %collective-permute-start.23) | collective-permute-done | bytes 4194336 | tf_op jit(solution)/shard_map/ppermute | solution.py:42
  804.0 1.5 collective-permute-start.25
  805.5 3.4 add_convert_fusion
  808.8 0.5 collective-permute-start.19
  809.4 1.3 collective-permute-start.31
  810.7 0.5 collective-permute-start.30
  811.2 64.1 %collective-permute-done.25.refs_2_.refs_6_ = bf16[1024,2048]{1,0:T(8,128)(2,1)} collective-permute-done((bf16[1024,2048]{1,0:T(8,128)(2,1)}, bf16[1024,2048]{1,0:T(8,128)(2,1)}, u32[]{:S(2)}, u32[]{:S(2)}) %collective-permute-start.25) | collective-permute-done | bytes 4194336 | tf_op jit(solution)/shard_map/ppermute | solution.py:42
  875.3 1.3 copy-done.3
  876.6 0.5 collective-permute-start.26
  877.1 44.4 %shard_map.88 = (f32[2,2048,2048]{2,1,0:T(8,128)}, f32[8,128]{1,0:T(8,128)}) custom-call(s32[6]{0:T(128)} %stack.27.order_ref, bf16[2,4,1024,2048]{3,2,1,0:T(8,128)(2,1)} %bitcast.21, bf16[2,4,1024,2048]{3,2,1,0:T(8,128)(2,1)} %bitcast.22, bf16[2,4,1024,2048]{3,2,1,0:T(8,128)(2,1)} %bitcast.23, ...), custom_call_target="tpu_custom_call", output_to_operand_aliasing={{0}: (9, {})} | custom-call | flops 34359738368 | bytes 60000000 | tf_op jit(solution)/shard_map/pallas_call | solution.py:68
  921.4 5.2 maximum_select_fusion.1.refs_9_
  926.6 1.3 collective-permute-start.22
  927.9 1.5 collective-permute-start.20
  929.4 43.3 %shard_map.89 = (bf16[4,1024,2048]{2,1,0:T(8,128)(2,1)}, f32[8,128]{1,0:T(8,128)}) custom-call(s32[6]{0:T(128)} %stack.27.order_ref, bf16[1024,2048]{1,0:T(8,128)(2,1)} %collective-permute-done.27.refs_0_, bf16[1024,2048]{1,0:T(8,128)(2,1)} %collective-permute-done.28.refs_1_, bf16[1024,2048]{1,0:T(8,128)(2,1)} %collective-permute-done.29.refs_2_, ...), custom_call_target="tpu_custom_call" | custom-call | flops 34359738368 | bytes 60000000 | tf_op jit(solution)/shard_map/pallas_call | solution.py:68
  972.7 20.3 %collective-permute-done.31.refs_9_ = f32[1024,2048]{1,0:T(8,128)} collective-permute-done((f32[1024,2048]{1,0:T(8,128)}, f32[1024,2048]{1,0:T(8,128)}, u32[]{:S(2)}, u32[]{:S(2)}) %collective-permute-start.31) | collective-permute-done | bytes 8388640 | tf_op jit(solution)/shard_map/ppermute | solution.py:42
  993.0 58.9 %shard_map.90 = (bf16[4,1024,2048]{2,1,0:T(8,128)(2,1)}, bf16[2,1024,2048]{2,1,0:T(8,128)(2,1)}, bf16[2,1024,2048]{2,1,0:T(8,128)(2,1)}, f32[2,2048,2048]{2,1,0:T(8,128)}, f32[8,128]{1,0:T(8,128)}) custom-call(s32[6]{0:T(128)} %stack.27.order_ref, bf16[1024,2048]{1,0:T(8,128)(2,1)} %collective-permute-done.23.refs_0_.refs_4_, ...), custom_call_target="tpu_custom_call", output_to_operand_aliasing={{3}: (11, {})} | custom-call | flops 34359738368 | bytes 60000000 | tf_op jit(solution)/shard_map/pallas_call | solution.py:68
  1052.0 45.5 %shard_map.91 = (f32[2,2048,2048]{2,1,0:T(8,128)}, f32[8,128]{1,0:T(8,128)}) custom-call(s32[6]{0:T(128)} %stack.27.order_ref, bf16[1024,2048]{1,0:T(8,128)(2,1)} %collective-permute-done.27.refs_0_, bf16[1024,2048]{1,0:T(8,128)(2,1)} %collective-permute-done.28.refs_1_, ...), custom_call_target="tpu_custom_call", output_to_operand_aliasing={{0}: (9, {})} | custom-call | flops 34359738368 | bytes 60000000 | tf_op jit(solution)/shard_map/pallas_call | solution.py:68
  1097.5 51.4 %shard_map.92 = (f32[2,2048,2048]{2,1,0:T(8,128)}, bf16[4,1024,2048]{2,1,0:T(8,128)(2,1)}, f32[8,128]{1,0:T(8,128)}) custom-call(s32[6]{0:T(128)} %stack.27.order_ref, bf16[4,1024,2048]{2,1,0:T(8,128)(2,1)} %get-tuple-element.94.refs_0_.refs_1_.refs_2_.refs_3_, ...), custom_call_target="tpu_custom_call", output_to_operand_aliasing={{0}: (9, {})} | custom-call | flops 34359738368 | bytes 60000000 | tf_op jit(solution)/shard_map/pallas_call | solution.py:68
  1148.9 22.1 %collective-permute-done.22.refs_1_ = f32[2048,1024]{1,0:T(8,128)} collective-permute-done((f32[2048,1024]{1,0:T(8,128)}, f32[2048,1024]{1,0:T(8,128)}, u32[]{:S(2)}, u32[]{:S(2)}) %collective-permute-start.22) | collective-permute-done | bytes 8388640 | tf_op jit(solution)/shard_map/ppermute | solution.py:42
  1170.9 10.0 shard_map.93
  (39 shorter events, 1.1 us)
Async XLA Ops:
  0.6 95.2 %collective-permute-start.1 = (bf16[2,2048,2048]{2,1,0:T(8,128)(2,1)}, bf16[2,2048,2048]{2,1,0:T(8,128)(2,1)}, u32[]{:S(2)}, u32[]{:S(2)}) collective-permute-start(bf16[2,2048,2048]{2,1,0:T(8,128)(2,1)} %refs_4_.11), channel_id=1, source_target_pairs={{0,1},{1,0},{2,3},{3,2},{4,5},{5,4},{6,7},{7,6},{8,9},{9,8},{10,11... | collective-permute-start | bytes 50331656 | tf_op jit(solution)/shard_map/ppermute | solution.py:42
  62.4 33.3 %collective-permute-start = (bf16[2,1024,2048]{2,1,0:T(8,128)(2,1)}, bf16[2,1024,2048]{2,1,0:T(8,128)(2,1)}, u32[]{:S(2)}, u32[]{:S(2)}) collective-permute-start(bf16[2,1024,2048]{2,1,0:T(8,128)(2,1)} %get-tuple-element.57.refs_6_.refs_7_), channel_id=1, source_target_pairs={{0,1},{1,0},{2,3},{3,2},{4,5},{5,4},{6,7},{7,6},{8,9},{9,8},{10,11... | collective-permute-start | bytes 25165832 | tf_op jit(solution)/shard_map/ppermute | solution.py:42
  67.3 94.7 %collective-permute-start.8 = (bf16[1024,2048]{1,0:T(8,128)(2,1)}, bf16[1024,2048]{1,0:T(8,128)(2,1)}, u32[]{:S(2)}, u32[]{:S(2)}) collective-permute-start(bf16[1024,2048]{1,0:T(8,128)(2,1)} %dynamic-slice_bitcast_fusion.1), channel_id=1, source_target_pairs={{0,8},{1,9},{2,10},{3,11},{4,12},{5,13},{6,14},{7,15},{8,0},{9,1},... | collective-permute-start | bytes 12582920 | tf_op jit(solution)/shard_map/ppermute | solution.py:42
  139.4 48.9 %collective-permute-start.2 = (bf16[1024,2048]{1,0:T(8,128)(2,1)}, bf16[1024,2048]{1,0:T(8,128)(2,1)}, u32[]{:S(2)}, u32[]{:S(2)}) collective-permute-start(bf16[1024,2048]{1,0:T(8,128)(2,1)} %get-tuple-element.62), channel_id=1, source_target_pairs={{0,2},{1,5},{2,0},{3,7},{4,6},{5,1},{6,4},{7,3},{8,10},{9,13},{10,... | collective-permute-start | bytes 12582920 | tf_op jit(solution)/shard_map/ppermute | solution.py:42
  140.9 110.4 %collective-permute-start.12 = (bf16[1024,2048]{1,0:T(8,128)(2,1)}, bf16[1024,2048]{1,0:T(8,128)(2,1)}, u32[]{:S(2)}, u32[]{:S(2)}) collective-permute-start(bf16[1024,2048]{1,0:T(8,128)(2,1)} %get-tuple-element.55), channel_id=1, source_target_pairs={{0,8},{1,9},{2,10},{3,11},{4,12},{5,13},{6,14},{7,15},{8,0},{9,1},... | collective-permute-start | bytes 12582920 | tf_op jit(solution)/shard_map/ppermute | solution.py:42
  162.1 97.8 %collective-permute-start.10 = (bf16[1024,2048]{1,0:T(8,128)(2,1)}, bf16[1024,2048]{1,0:T(8,128)(2,1)}, u32[]{:S(2)}, u32[]{:S(2)}) collective-permute-start(bf16[1024,2048]{1,0:T(8,128)(2,1)} %collective-permute-done.8.refs_0_), channel_id=1, source_target_pairs={{0,2},{1,5},{2,0},{3,7},{4,6},{5,1},{6,4},{7,3},{8,10},{9,13},{10,... | collective-permute-start | bytes 12582920 | tf_op jit(solution)/shard_map/ppermute | solution.py:42
  191.3 61.7 %collective-permute-start.3 = (bf16[512,2048]{1,0:T(8,128)(2,1)S(1)}, bf16[512,2048]{1,0:T(8,128)(2,1)}, u32[]{:S(2)}, u32[]{:S(2)}) collective-permute-start(bf16[512,2048]{1,0:T(8,128)(2,1)S(1)} %add_convert_fusion.3), channel_id=1, source_target_pairs={{0,4},{1,3},{2,6},{3,1},{4,0},{5,7},{6,2},{7,5},{8,12},{9,11},{10,... | collective-permute-start | bytes 6291464 | tf_op jit(solution)/shard_map/ppermute | solution.py:42
  251.3 71.7 %collective-permute-start.14 = (bf16[1024,2048]{1,0:T(8,128)(2,1)}, bf16[1024,2048]{1,0:T(8,128)(2,1)}, u32[]{:S(2)}, u32[]{:S(2)}) collective-permute-start(bf16[1024,2048]{1,0:T(8,128)(2,1)} %collective-permute-done.12.refs_0_.refs_4_), channel_id=1, source_target_pairs={{0,2},{1,5},{2,0},{3,7},{4,6},{5,1},{6,4},{7,3},{8,10},{9,13},{10,... | collective-permute-start | bytes 12582920 | tf_op jit(solution)/shard_map/ppermute | solution.py:42
  258.3 53.9 %copy-start = (bf16[512,2048]{1,0:T(8,128)(2,1)}, bf16[512,2048]{1,0:T(8,128)(2,1)S(1)}, u32[]{:S(2)}) copy-start(bf16[512,2048]{1,0:T(8,128)(2,1)S(1)} %add_convert_fusion.2) | copy-start | bytes 6291460
  258.3 48.6 %collective-permute-start.4 = (bf16[512,2048]{1,0:T(8,128)(2,1)S(1)}, bf16[512,2048]{1,0:T(8,128)(2,1)}, u32[]{:S(2)}, u32[]{:S(2)}) collective-permute-start(bf16[512,2048]{1,0:T(8,128)(2,1)S(1)} %add_convert_fusion.2), channel_id=1, source_target_pairs={{0,4},{1,3},{2,6},{3,1},{4,0},{5,7},{6,2},{7,5},{8,12},{9,11},{10,... | collective-permute-start | bytes 6291464 | tf_op jit(solution)/shard_map/ppermute | solution.py:42
  259.8 63.3 %collective-permute-start.9 = (bf16[1024,2048]{1,0:T(8,128)(2,1)}, bf16[1024,2048]{1,0:T(8,128)(2,1)}, u32[]{:S(2)}, u32[]{:S(2)}) collective-permute-start(bf16[1024,2048]{1,0:T(8,128)(2,1)} %collective-permute-done.8.refs_0_), channel_id=1, source_target_pairs={{0,1},{1,0},{2,3},{3,2},{4,5},{5,4},{6,7},{7,6},{8,9},{9,8},{10,11... | collective-permute-start | bytes 12582920 | tf_op jit(solution)/shard_map/ppermute | solution.py:42
  259.8 63.3 %collective-permute-start.11 = (bf16[1024,2048]{1,0:T(8,128)(2,1)}, bf16[1024,2048]{1,0:T(8,128)(2,1)}, u32[]{:S(2)}, u32[]{:S(2)}) collective-permute-start(bf16[1024,2048]{1,0:T(8,128)(2,1)} %collective-permute-done.10.refs_2_), channel_id=1, source_target_pairs={{0,1},{1,0},{2,3},{3,2},{4,5},{5,4},{6,7},{7,6},{8,9},{9,8},{10,11... | collective-permute-start | bytes 12582920 | tf_op jit(solution)/shard_map/ppermute | solution.py:42
  260.3 86.4 %collective-permute-start.13 = (bf16[1024,2048]{1,0:T(8,128)(2,1)}, bf16[1024,2048]{1,0:T(8,128)(2,1)}, u32[]{:S(2)}, u32[]{:S(2)}) collective-permute-start(bf16[1024,2048]{1,0:T(8,128)(2,1)} %collective-permute-done.12.refs_0_.refs_4_), channel_id=1, source_target_pairs={{0,1},{1,0},{2,3},{3,2},{4,5},{5,4},{6,7},{7,6},{8,9},{9,8},{10,11... | collective-permute-start | bytes 12582920 | tf_op jit(solution)/shard_map/ppermute | solution.py:42
  312.1 55.9 %collective-permute-start.5 = (bf16[1024,2048]{1,0:T(8,128)(2,1)}, bf16[1024,2048]{1,0:T(8,128)(2,1)}, u32[]{:S(2)}, u32[]{:S(2)}) collective-permute-start(bf16[1024,2048]{1,0:T(8,128)(2,1)} %maximum_select_fusion.refs_0_.refs_4_), channel_id=1, source_target_pairs={{0,2},{1,5},{2,0},{3,7},{4,6},{5,1},{6,4},{7,3},{8,10},{9,13},{10,... | collective-permute-start | bytes 12582920 | tf_op jit(solution)/shard_map/ppermute | solution.py:42
  323.1 70.9 %collective-permute-start.15 = (bf16[1024,2048]{1,0:T(8,128)(2,1)}, bf16[1024,2048]{1,0:T(8,128)(2,1)}, u32[]{:S(2)}, u32[]{:S(2)}) collective-permute-start(bf16[1024,2048]{1,0:T(8,128)(2,1)} %collective-permute-done.14.refs_0_.refs_6_), channel_id=1, source_target_pairs={{0,1},{1,0},{2,3},{3,2},{4,5},{5,4},{6,7},{7,6},{8,9},{9,8},{10,11... | collective-permute-start | bytes 12582920 | tf_op jit(solution)/shard_map/ppermute | solution.py:42
  364.9 104.3 %collective-permute-start.6 = (bf16[1024,2048]{1,0:T(8,128)(2,1)}, bf16[1024,2048]{1,0:T(8,128)(2,1)}, u32[]{:S(2)}, u32[]{:S(2)}) collective-permute-start(bf16[1024,2048]{1,0:T(8,128)(2,1)} %maximum_select_fusion.refs_0_.refs_4_), channel_id=1, source_target_pairs={{0,1},{1,0},{2,3},{3,2},{4,5},{5,4},{6,7},{7,6},{8,9},{9,8},{10,11... | collective-permute-start | bytes 12582920 | tf_op jit(solution)/shard_map/ppermute | solution.py:42
  368.0 101.2 %collective-permute-start.7 = (bf16[1024,2048]{1,0:T(8,128)(2,1)}, bf16[1024,2048]{1,0:T(8,128)(2,1)}, u32[]{:S(2)}, u32[]{:S(2)}) collective-permute-start(bf16[1024,2048]{1,0:T(8,128)(2,1)} %collective-permute-done.5.refs_1_.refs_5_), channel_id=1, source_target_pairs={{0,1},{1,0},{2,3},{3,2},{4,5},{5,4},{6,7},{7,6},{8,9},{9,8},{10,11... | collective-permute-start | bytes 12582920 | tf_op jit(solution)/shard_map/ppermute | solution.py:42
  527.4 44.6 %collective-permute-start.16 = (bf16[2,1024,2048]{2,1,0:T(8,128)(2,1)}, bf16[2,1024,2048]{2,1,0:T(8,128)(2,1)}, u32[]{:S(2)}, u32[]{:S(2)}) collective-permute-start(bf16[2,1024,2048]{2,1,0:T(8,128)(2,1)} %get-tuple-element.79.refs_6_.refs_7_), channel_id=1, source_target_pairs={{0,1},{1,0},{2,3},{3,2},{4,5},{5,4},{6,7},{7,6},{8,9},{9,8},{10,11... | collective-permute-start | bytes 25165832 | tf_op jit(solution)/shard_map/ppermute | solution.py:42
  615.6 48.8 %collective-permute-start.17 = (bf16[1024,2048]{1,0:T(8,128)(2,1)}, bf16[1024,2048]{1,0:T(8,128)(2,1)}, u32[]{:S(2)}, u32[]{:S(2)}) collective-permute-start(bf16[1024,2048]{1,0:T(8,128)(2,1)} %get-tuple-element.85), channel_id=1, source_target_pairs={{0,2},{1,5},{2,0},{3,7},{4,6},{5,1},{6,4},{7,3},{8,10},{9,13},{10,... | collective-permute-start | bytes 12582920 | tf_op jit(solution)/shard_map/ppermute | solution.py:42
  619.0 45.4 %copy-start.2 = (bf16[1024,2048]{1,0:T(8,128)(2,1)S(1)}, bf16[1024,2048]{1,0:T(8,128)(2,1)}, u32[]{:S(2)}) copy-start(bf16[1024,2048]{1,0:T(8,128)(2,1)} %get-tuple-element.84) | copy-start | bytes 12582916
  621.7 183.8 %copy-start.1 = (bf16[512,2048]{1,0:T(8,128)(2,1)S(1)}, bf16[512,2048]{1,0:T(8,128)(2,1)}, u32[]{:S(2)}) copy-start(bf16[512,2048]{1,0:T(8,128)(2,1)} %copy-done) | copy-start | bytes 6291460
  621.7 93.6 %collective-permute-start.27 = (bf16[1024,2048]{1,0:T(8,128)(2,1)S(1)}, bf16[1024,2048]{1,0:T(8,128)(2,1)}, u32[]{:S(2)}, u32[]{:S(2)}) collective-permute-start(bf16[1024,2048]{1,0:T(8,128)(2,1)S(1)} %dynamic-slice_bitcast_fusion), channel_id=1, source_target_pairs={{0,8},{1,9},{2,10},{3,11},{4,12},{5,13},{6,14},{7,15},{8,0},{9,1},... | collective-permute-start | bytes 12582920 | tf_op jit(solution)/shard_map/ppermute | solution.py:42
  623.0 181.0 %collective-permute-start.23 = (bf16[1024,2048]{1,0:T(8,128)(2,1)}, bf16[1024,2048]{1,0:T(8,128)(2,1)}, u32[]{:S(2)}, u32[]{:S(2)}) collective-permute-start(bf16[1024,2048]{1,0:T(8,128)(2,1)} %maximum_select_fusion.refs_0_.refs_4_), channel_id=1, source_target_pairs={{0,8},{1,9},{2,10},{3,11},{4,12},{5,13},{6,14},{7,15},{8,0},{9,1},... | collective-permute-start | bytes 12582920 | tf_op jit(solution)/shard_map/ppermute | solution.py:42
  666.8 138.6 %collective-permute-start.18 = (bf16[512,2048]{1,0:T(8,128)(2,1)S(1)}, bf16[512,2048]{1,0:T(8,128)(2,1)S(1)}, u32[]{:S(2)}, u32[]{:S(2)}) collective-permute-start(bf16[512,2048]{1,0:T(8,128)(2,1)S(1)} %add_convert_fusion.1), channel_id=1, source_target_pairs={{0,4},{1,3},{2,6},{3,1},{4,0},{5,7},{6,2},{7,5},{8,12},{9,11},{10,... | collective-permute-start | bytes 6291464 | tf_op jit(solution)/shard_map/ppermute | solution.py:42
  715.3 95.4 %collective-permute-start.29 = (bf16[1024,2048]{1,0:T(8,128)(2,1)}, bf16[1024,2048]{1,0:T(8,128)(2,1)}, u32[]{:S(2)}, u32[]{:S(2)}) collective-permute-start(bf16[1024,2048]{1,0:T(8,128)(2,1)} %collective-permute-done.27.refs_0_), channel_id=1, source_target_pairs={{0,2},{1,5},{2,0},{3,7},{4,6},{5,1},{6,4},{7,3},{8,10},{9,13},{10,... | collective-permute-start | bytes 12582920 | tf_op jit(solution)/shard_map/ppermute | solution.py:42
  804.0 71.3 %collective-permute-start.25 = (bf16[1024,2048]{1,0:T(8,128)(2,1)}, bf16[1024,2048]{1,0:T(8,128)(2,1)}, u32[]{:S(2)}, u32[]{:S(2)}) collective-permute-start(bf16[1024,2048]{1,0:T(8,128)(2,1)} %collective-permute-done.23.refs_0_.refs_4_), channel_id=1, source_target_pairs={{0,2},{1,5},{2,0},{3,7},{4,6},{5,1},{6,4},{7,3},{8,10},{9,13},{10,... | collective-permute-start | bytes 12582920 | tf_op jit(solution)/shard_map/ppermute | solution.py:42
  808.8 66.4 %collective-permute-start.19 = (bf16[512,2048]{1,0:T(8,128)(2,1)S(1)}, bf16[512,2048]{1,0:T(8,128)(2,1)S(1)}, u32[]{:S(2)}, u32[]{:S(2)}) collective-permute-start(bf16[512,2048]{1,0:T(8,128)(2,1)S(1)} %add_convert_fusion), channel_id=1, source_target_pairs={{0,4},{1,3},{2,6},{3,1},{4,0},{5,7},{6,2},{7,5},{8,12},{9,11},{10,... | collective-permute-start | bytes 6291464 | tf_op jit(solution)/shard_map/ppermute | solution.py:42
  809.4 183.6 %collective-permute-start.31 = (f32[1024,2048]{1,0:T(8,128)}, f32[1024,2048]{1,0:T(8,128)}, u32[]{:S(2)}, u32[]{:S(2)}) collective-permute-start(f32[1024,2048]{1,0:T(8,128)} %get-tuple-element.91), channel_id=1, source_target_pairs={{0,8},{1,9},{2,10},{3,11},{4,12},{5,13},{6,14},{7,15},{8,0},{9,1},... | collective-permute-start | bytes 25165832 | tf_op jit(solution)/shard_map/ppermute | solution.py:42
  810.7 116.0 %collective-permute-start.28 = (bf16[1024,2048]{1,0:T(8,128)(2,1)}, bf16[1024,2048]{1,0:T(8,128)(2,1)}, u32[]{:S(2)}, u32[]{:S(2)}) collective-permute-start(bf16[1024,2048]{1,0:T(8,128)(2,1)} %collective-permute-done.27.refs_0_), channel_id=1, source_target_pairs={{0,1},{1,0},{2,3},{3,2},{4,5},{5,4},{6,7},{7,6},{8,9},{9,8},{10,11... | collective-permute-start | bytes 12582920 | tf_op jit(solution)/shard_map/ppermute | solution.py:42
  810.7 117.2 %collective-permute-start.30 = (bf16[1024,2048]{1,0:T(8,128)(2,1)}, bf16[1024,2048]{1,0:T(8,128)(2,1)}, u32[]{:S(2)}, u32[]{:S(2)}) collective-permute-start(bf16[1024,2048]{1,0:T(8,128)(2,1)} %collective-permute-done.29.refs_2_), channel_id=1, source_target_pairs={{0,1},{1,0},{2,3},{3,2},{4,5},{5,4},{6,7},{7,6},{8,9},{9,8},{10,11... | collective-permute-start | bytes 12582920 | tf_op jit(solution)/shard_map/ppermute | solution.py:42
  875.2 97.4 %collective-permute-start.24 = (bf16[1024,2048]{1,0:T(8,128)(2,1)}, bf16[1024,2048]{1,0:T(8,128)(2,1)}, u32[]{:S(2)}, u32[]{:S(2)}) collective-permute-start(bf16[1024,2048]{1,0:T(8,128)(2,1)} %collective-permute-done.23.refs_0_.refs_4_), channel_id=1, source_target_pairs={{0,1},{1,0},{2,3},{3,2},{4,5},{5,4},{6,7},{7,6},{8,9},{9,8},{10,11... | collective-permute-start | bytes 12582920 | tf_op jit(solution)/shard_map/ppermute | solution.py:42
  875.3 1.3 copy-start.3
  876.6 116.5 %collective-permute-start.26 = (bf16[1024,2048]{1,0:T(8,128)(2,1)}, bf16[1024,2048]{1,0:T(8,128)(2,1)}, u32[]{:S(2)}, u32[]{:S(2)}) collective-permute-start(bf16[1024,2048]{1,0:T(8,128)(2,1)} %collective-permute-done.25.refs_2_.refs_6_), channel_id=1, source_target_pairs={{0,1},{1,0},{2,3},{3,2},{4,5},{5,4},{6,7},{7,6},{8,9},{9,8},{10,11... | collective-permute-start | bytes 12582920 | tf_op jit(solution)/shard_map/ppermute | solution.py:42
  926.6 244.3 %collective-permute-start.22 = (f32[2048,1024]{1,0:T(8,128)}, f32[2048,1024]{1,0:T(8,128)}, u32[]{:S(2)}, u32[]{:S(2)}) collective-permute-start(f32[2048,1024]{1,0:T(8,128)} %get-tuple-element.86), channel_id=1, source_target_pairs={{0,8},{1,9},{2,10},{3,11},{4,12},{5,13},{6,14},{7,15},{8,0},{9,1},... | collective-permute-start | bytes 25165832 | tf_op jit(solution)/shard_map/ppermute | solution.py:42
  927.9 124.0 %collective-permute-start.20 = (bf16[1024,2048]{1,0:T(8,128)(2,1)}, bf16[1024,2048]{1,0:T(8,128)(2,1)}, u32[]{:S(2)}, u32[]{:S(2)}) collective-permute-start(bf16[1024,2048]{1,0:T(8,128)(2,1)} %maximum_select_fusion.1.refs_9_), channel_id=1, source_target_pairs={{0,2},{1,5},{2,0},{3,7},{4,6},{5,1},{6,4},{7,3},{8,10},{9,13},{10,... | collective-permute-start | bytes 12582920 | tf_op jit(solution)/shard_map/ppermute | solution.py:42
  972.7 124.8 %collective-permute-start.32 = (bf16[1024,2048]{1,0:T(8,128)(2,1)}, bf16[1024,2048]{1,0:T(8,128)(2,1)}, u32[]{:S(2)}, u32[]{:S(2)}) collective-permute-start(bf16[1024,2048]{1,0:T(8,128)(2,1)} %maximum_select_fusion.1.refs_9_), channel_id=1, source_target_pairs={{0,1},{1,0},{2,3},{3,2},{4,5},{5,4},{6,7},{7,6},{8,9},{9,8},{10,11... | collective-permute-start | bytes 12582920 | tf_op jit(solution)/shard_map/ppermute | solution.py:42
  1051.9 119.0 %collective-permute-start.21 = (bf16[1024,2048]{1,0:T(8,128)(2,1)}, bf16[1024,2048]{1,0:T(8,128)(2,1)}, u32[]{:S(2)}, u32[]{:S(2)}) collective-permute-start(bf16[1024,2048]{1,0:T(8,128)(2,1)} %collective-permute-done.20.refs_10_), channel_id=1, source_target_pairs={{0,1},{1,0},{2,3},{3,2},{4,5},{5,4},{6,7},{7,6},{8,9},{9,8},{10,11... | collective-permute-start | bytes 12582920 | tf_op jit(solution)/shard_map/ppermute | solution.py:42
